TPU v7x, 32 devices: a whole 2x2x4 slice. The times are simulated.
32 devices in a mesh: section: 2 (over y), dp: 4 (over x, core), mp: 4 (over z).
Axes of the slice: x: 2, y: 2, z: 4, core: 2. Of those that a mesh axis runs over, the one named last changes fastest.
Arguments:
- patches: bfloat16 [4096, 1280], P(('section', 'dp')), may hold values from -6 to 6
- patch_counts: int32 [16], P(('section', 'dp')), may hold values from 64 to 256, as said below
- dest_rows: int32 [1024], P(('section', 'dp')), may hold values from 0 to 4095, as said below
- qkv_weight: bfloat16 [1280, 3, 1280], P(None, None, 'mp'), may hold values from -1 to 1
- out_weight: bfloat16 [1280, 1280], P('mp'), may hold values from -0.15625 to 0.15625
- attn_gain: bfloat16 [1280], replicated, may hold values from 0.25 to 1.75
- merge_gain: bfloat16 [1280], replicated, may hold values from 0.25 to 1.75
- fc1_weight: bfloat16 [5120, 5120], P('mp', ('section', 'dp')), may hold values from -0.078125 to 0.078125
- fc1_bias: bfloat16 [5120], P(('section', 'dp')), may hold values from -3 to 3
- fc2_weight: bfloat16 [5120, 8192], P(('section', 'dp'), 'mp'), may hold values from -0.078125 to 0.078125
- fc2_bias: bfloat16 [8192], P('mp'), may hold values from -3 to 3
- text_embeds: bfloat16 [4096, 8192], P(('section', 'dp'), 'mp'), may hold values from -6 to 6
- section_hidden: bfloat16 [4096, 8192], P(('section', 'dp'), 'mp'), may hold values from -80 to 80
- llm_gain: bfloat16 [8192], P('mp'), may hold values from 0.25 to 1.75
Outputs:
- sequence_embeds: bfloat16 [4096, 8192], P(('section', 'dp'), 'mp')
- layer_inputs: bfloat16 [4096, 8192], P(('section', 'dp'), 'mp')
Inputs may be any that keep to these rules, and one draw needn't show every extreme that they name: `patch_counts`: multiples of 4; a tile's patches fill the first slots of its block. `dest_rows`: all rows differ. Each group's merged slots form runs of 16 consecutive slots (aligned); a run goes to one sequence slice (row // 512, numbered in section-major order), different runs of a group to different slices. Rows of slots that are not live are never written.
All inputs are finite; a program needn't handle non-finite values.
Results may differ from a plain program's by a relative error of at most 0.0055.
Values may be sent and summed in bfloat16 or wider, within the bound.
A program may use at most 128 MiB of HBM per device.

v0:
```python
import jax
import jax.numpy as jnp
from jax import lax
from jax.sharding import PartitionSpec as P

HEAD_DIM = 80
HID = 8192


vit_eps = 1e-06
llm_eps = 1e-06


def from_behind(value, axis, steps):
    count = lax.axis_size(axis)
    first, last = (max(0, -steps), min(count, count - steps))
    return lax.ppermute(value, axis, [(source, source + steps) for source in range(first, last)])


def layer_norm(values, gain):
    centred = values.astype(jnp.float32)
    centred = centred - jnp.mean(centred, axis=-1, keepdims=True)
    variance = jnp.mean(centred * centred, axis=-1, keepdims=True)
    return centred * lax.rsqrt(variance + vit_eps) * gain.astype(jnp.float32)


def per_device(
    patches,
    patch_counts,
    dest_rows,
    qkv_weight,
    out_weight,
    attn_gain,
    merge_gain,
    fc1_weight,
    fc1_bias,
    fc2_weight,
    fc2_bias,
    text_embeds,
    section_hidden,
    llm_gain,
):
    width = patches.shape[1]
    tile_total = patch_counts.shape[0]
    block_rows = patches.shape[0] // tile_total
    merged_rows = patches.shape[0] // 4
    local_cols = qkv_weight.shape[2]
    local_heads = local_cols // HEAD_DIM
    feature_cols = text_embeds.shape[1]
    seq_rows = text_embeds.shape[0]
    section_count = lax.axis_size("section")
    group_count = section_count * lax.axis_size("dp")
    run_cap = max(2, merged_rows // group_count)
    run_total = merged_rows // run_cap
    normed_in = layer_norm(patches, attn_gain).astype(jnp.bfloat16)
    projections = jnp.dot(
        normed_in, qkv_weight.reshape(width, 3 * local_cols), preferred_element_type=jnp.float32
    ).astype(jnp.bfloat16)
    projections = projections.reshape(tile_total, block_rows, 3, local_heads, HEAD_DIM)
    query_part = projections[:, :, 0]
    key_part = projections[:, :, 1]
    value_part = projections[:, :, 2]
    scores = jnp.einsum(
        "tqhd,tkhd->thqk", query_part, key_part, preferred_element_type=jnp.float32
    ) * HEAD_DIM ** (-0.5)
    key_live = (
        jnp.arange(block_rows, dtype=jnp.int32)[None, None, None, :]
        < patch_counts[:, None, None, None]
    )
    scores = jnp.where(key_live, scores, -1e30)
    weights = jax.nn.softmax(scores, axis=-1).astype(jnp.bfloat16)
    attended = jnp.einsum(
        "thqk,tkhd->tqhd", weights, value_part, preferred_element_type=jnp.float32
    ).astype(jnp.bfloat16)
    attended = attended.reshape(patches.shape[0], local_cols)
    partial_proj = jnp.dot(attended, out_weight, preferred_element_type=jnp.float32)
    position = lax.axis_index("mp")
    own_patch = lax.dynamic_slice_in_dim(
        patches.reshape(merged_rows, 4, width), position, 1, 1
    ).reshape(merged_rows, width)
    own_proj = lax.psum_scatter(
        partial_proj.reshape(merged_rows, 4, width), "mp", scatter_dimension=1, tiled=True
    ).reshape(merged_rows, width)
    block_out = (own_patch.astype(jnp.float32) + own_proj).astype(jnp.bfloat16)
    merge_part = layer_norm(block_out, merge_gain).astype(jnp.bfloat16)
    first_full, second_full, bias_full = (
        lax.all_gather(fc1_weight, "section", axis=1, tiled=True),
        lax.all_gather(fc2_weight, "section", axis=0, tiled=True),
        lax.all_gather(fc1_bias, "section", axis=0, tiled=True),
    )
    first_partial = jnp.dot(
        lax.all_gather(merge_part, "dp", axis=0, tiled=True),
        first_full,
        preferred_element_type=jnp.float32,
    )
    first_total = lax.psum(first_partial, "mp")
    hidden = jax.nn.gelu(first_total + bias_full.astype(jnp.float32), approximate=False).astype(
        jnp.bfloat16
    )
    embed_total = lax.psum_scatter(
        jnp.dot(hidden, second_full, preferred_element_type=jnp.float32).astype(jnp.bfloat16),
        "dp",
        scatter_dimension=0,
        tiled=True,
    ).astype(jnp.float32)
    image_embeds = (embed_total + fc2_bias.astype(jnp.float32)).astype(jnp.bfloat16)
    slot_in_tile = jnp.arange(merged_rows, dtype=jnp.int32) % (block_rows // 4)
    tile_counts = jnp.repeat(patch_counts, block_rows // 4, total_repeat_length=merged_rows)
    live = slot_in_tile * 4 < tile_counts
    receiver = dest_rows // seq_rows
    run_target = receiver.reshape(run_total, run_cap)[:, 0]
    place = jnp.where(live, dest_rows % seq_rows, seq_rows)
    send_rows = (
        jnp.zeros((group_count, run_cap, feature_cols), jnp.bfloat16)
        .at[run_target]
        .set(image_embeds.reshape(run_total, run_cap, feature_cols))
    )
    send_place = (
        jnp.full((group_count, run_cap), seq_rows, jnp.int32)
        .at[run_target]
        .set(place.reshape(run_total, run_cap))
    )
    got_rows, got_place = (
        lax.all_to_all(send_rows, ("section", "dp"), split_axis=0, concat_axis=0, tiled=True),
        lax.all_to_all(send_place, ("section", "dp"), split_axis=0, concat_axis=0, tiled=True),
    )
    sequence_embeds = text_embeds.at[got_place.reshape(-1)].set(
        got_rows.reshape(-1, feature_cols), mode="drop"
    )
    incoming = from_behind(section_hidden, "section", 1)
    entering = jnp.where(lax.axis_index("section") == 0, sequence_embeds, incoming).astype(
        jnp.float32
    )
    row_total = lax.psum(jnp.sum(entering * entering, axis=1), "mp")
    layer_inputs = (
        entering * lax.rsqrt(row_total / HID + llm_eps)[:, None] * llm_gain.astype(jnp.float32)
    ).astype(jnp.bfloat16)
    return (sequence_embeds, layer_inputs)


def solution(mesh):
    in_specs = (
        P(("section", "dp"), None),
        P(("section", "dp")),
        P(("section", "dp")),
        P(None, None, "mp"),
        P("mp", None),
        P(),
        P(),
        P("mp", ("section", "dp")),
        P(("section", "dp")),
        P(("section", "dp"), "mp"),
        P("mp"),
        P(("section", "dp"), "mp"),
        P(("section", "dp"), "mp"),
        P("mp"),
    )
    out_specs = (P(("section", "dp"), "mp"), P(("section", "dp"), "mp"))
    return jax.shard_map(
        per_device, mesh=mesh, in_specs=in_specs, out_specs=out_specs, check_vma=False
    )
```

profile of v0, /device:TPU:0, one launch (start us, length us, event | category | flops | bytes accessed | tf_op | source)
XLA Modules:
  0.0 317.5 jit_solution(10290408837068384715)
XLA Ops:
  8.0 0.0 copy-start
  8.0 0.0 reduce-scatter.3.cloned.1.call-start
  8.1 0.0 copy-start.1
  8.1 3.3 %copy.70 = bf16[512,2048]{1,0:T(8,128)(2,1)} copy(bf16[512,2048]{1,0:T(8,128)(2,1)} %param.27) | data formatting | bytes 4194304
  11.4 0.2 convert_reduce_fusion
  11.7 0.5 fusion.6
  12.2 2.6 convolution_convert_fusion.1
  14.8 2.5 reshape.162
  17.3 1.6 fusion.107
  18.9 0.1 iota_compare_fusion
  18.9 3.3 %fusion.109 = (f32[2,4,256]{2,1,0:T(4,128)S(1)}, f32[2,4,256,256]{2,3,1,0:T(8,128)}) fusion(pred[2,256]{1,0:T(4,128)(4,1)S(1)} %iota_compare_fusion, bf16[2,256,1,4,80]{1,0,4,3,2:T(2,128)(2,1)} %get-tuple-element.18, bf16[2,256,1,4,80]{1,0,4,3,2:T(2,128)(2,1)} %get-tuple-element.17), kind=kOutput, calls=%fused_computation.154 | convolution fusion | flops 85983488 | bytes 2761216 | tf_op jit(solution)/shard_map/sub | solution.py:71
  22.2 1.9 fusion.56
  24.1 0.3 copy.33
  24.4 0.5 dot_general.23
  24.9 3.5 %fusion.60 = f32[128,4,1280]{2,0,1:T(8,128)} fusion(bf16[320,1280]{1,0:T(8,128)(2,1)} %param.20, bf16[128,4,320]{2,1,0:T(4,128)(2,1)S(1)} %dot_general.23), kind=kOutput, calls=%fused_computation.82 | convolution fusion | flops 419430400 | bytes 3768320 | tf_op jit(solution)/shard_map/dot_general | solution.py:76
  28.4 0.0 reduce-scatter.3.cloned.1.call-update
  28.5 0.0 copy-start.4
  28.5 0.0 all-gather.7.cloned.1.call-start
  28.5 0.5 all-gather.7.cloned.1.call-update
  29.1 0.0 all-gather.5.cloned.1.call-start
  29.1 3.5 %reshape.160 = bf16[128,4,1280]{2,1,0:T(4,128)(2,1)} reshape(bf16[512,1280]{1,0:T(8,128)(2,1)} %param.16) | data formatting | bytes 2621440 | tf_op jit(solution)/shard_map/reshape | solution.py:79
  32.6 2.0 constant_dynamic-slice_fusion
  34.6 49.0 %reduce-scatter.3.cloned.1.call-done = f32[128,1,1280]{2,0,1:T(8,128)} async-done(((f32[128,4,1280]{2,0,1:T(8,128)}), f32[128,1,1280]{2,0,1:T(8,128)}) %reduce-scatter.3.cloned.1.call-update) | async-done | bytes 655376 | tf_op jit(solution)/shard_map/reduce_scatter | solution.py:81
  83.6 1.2 convert_reduce_fusion.1
  84.8 0.2 fusion.65
  85.1 1.0 fusion.67
  86.0 0.0 all-gather.5.cloned.1.call-update
  86.1 0.0 all-gather.9.cloned.1.call-start
  86.1 0.5 all-gather.9.cloned.1.call-update
  86.6 0.0 all-reduce.2.cloned.1.call-start
  86.7 0.0 all-gather.7.cloned.1.call-done
  86.7 17.1 %all-gather.5.cloned.1.call-done = bf16[512,1280]{1,0:T(8,128)(2,1)} async-done(((bf16[128,1280]{1,0:T(8,128)(2,1)}), bf16[512,1280]{1,0:T(8,128)(2,1)}) %all-gather.5.cloned.1.call-update) | async-done | bytes 1310736 | tf_op jit(solution)/shard_map/all_gather | solution.py:92
  103.8 5.8 %fusion.110 = f32[512,1280]{1,0:T(8,128)} fusion(bf16[512,1280]{1,0:T(8,128)(2,1)} %all-gather.5.cloned.1.call-done, bf16[1280,1280]{1,0:T(8,128)(2,1)} %all-gather.7.cloned.1.call-done), kind=kOutput, calls=%fused_computation.155 | convolution fusion | flops 1677721600 | bytes 7208960 | tf_op jit(solution)/shard_map/dot_general | solution.py:91
  109.6 0.0 all-reduce.2.cloned.1.call-update
  109.6 0.0 reduce-scatter.5.cloned.1.call-start
  109.6 0.6 copy-done.7
  110.2 4.5 %all-gather = bf16[2,1,640]{2,1,0:T(2,128)(2,1)S(1)} all-gather(bf16[1,1,640]{2,1,0:T(2,128)(2,1)S(1)} %reshape.198), channel_id=1, replica_groups=mesh['section'=2,'dp'=4,'mp'=4] {'section'}, dimensions={0}, use_global_device_ids=true | all-gather | bytes 3840 | tf_op jit(solution)/shard_map/all_gather | solution.py:89
  114.8 0.0 copy-start.10
  114.8 58.8 %all-gather.9.cloned.1.call-done = bf16[1280,2048]{1,0:T(8,128)(2,1)} async-done(((bf16[640,2048]{1,0:T(8,128)(2,1)}), bf16[1280,2048]{1,0:T(8,128)(2,1)}) %all-gather.9.cloned.1.call-update) | async-done | bytes 5242896 | tf_op jit(solution)/shard_map/all_gather | solution.py:88
  173.6 40.2 %all-reduce.2.cloned.1.call-done = f32[512,1280]{1,0:T(8,128)} async-done(((f32[512,1280]{1,0:T(8,128)}), f32[512,1280]{1,0:T(8,128)}) %all-reduce.2.cloned.1.call-update) | async-done | bytes 2621456 | tf_op jit(solution)/shard_map/psum | solution.py:96
  213.8 12.1 %convolution_convert_fusion = bf16[512,2048]{1,0:T(8,128)(2,1)} fusion(bf16[1280,2048]{1,0:T(8,128)(2,1)} %all-gather.9.cloned.1.call-done, f32[512,1280]{1,0:T(8,128)} %all-reduce.2.cloned.1.call-done, f32[1280]{0:T(1024)S(1)} %reshape.200), kind=kOutput, calls=%fused_computation.14 | convolution fusion | flops 2728656896 | bytes 9966592 | tf_op jit(solution)/shard_map/dot_general | solution.py:101
  225.9 0.0 reduce-scatter.5.cloned.1.call-update
  225.9 4.7 %collective-permute-start = (bf16[512,2048]{1,0:T(8,128)(2,1)}, bf16[512,2048]{1,0:T(8,128)(2,1)}, u32[]{:S(2)}, u32[]{:S(2)}) collective-permute-start(bf16[512,2048]{1,0:T(8,128)(2,1)} %param.28), channel_id=1, source_target_pairs={{0,16},{1,17},{2,18},{3,19},{4,20},{5,21},{6,22},{7,23},{8,24},{9,... | collective-permute-start | bytes 6291464 | tf_op jit(solution)/shard_map/ppermute | solution.py:17
  230.7 0.6 fusion.108
  231.3 1.3 compare_select_fusion.2
  232.6 0.1 reshape.157
  232.6 0.1 reshape.178
  232.7 0.1 fusion.70
  232.8 1.2 scatter_custom_fusion
  234.0 3.3 %all-to-all-start = ((s32[8,1,16]{2,1,0:T(1,128)}), s32[8,1,16]{2,1,0:T(1,128)S(1)}, u32[]{:S(2)}, u32[]{:S(2)}) async-start(s32[8,1,16]{2,1,0:T(1,128)} %bitcast.3), calls=%async_computation | async-start | bytes 8192 | tf_op jit(solution)/shard_map/all_to_all | solution.py:125
  237.3 19.0 %reduce-scatter.5.cloned.1.call-done = bf16[128,2048]{1,0:T(8,128)(2,1)} async-done(((bf16[512,2048]{1,0:T(8,128)(2,1)}), bf16[128,2048]{1,0:T(8,128)(2,1)}) %reduce-scatter.5.cloned.1.call-update) | async-done | bytes 524304 | tf_op jit(solution)/shard_map/reduce_scatter | solution.py:100
  256.3 1.1 add_convert_fusion
  257.4 0.8 broadcast_in_dim.20
  258.3 2.4 scatter_fusion
  260.7 13.7 %all-to-all-done = s32[8,1,16]{2,1,0:T(1,128)S(1)} async-done(((s32[8,1,16]{2,1,0:T(1,128)}), s32[8,1,16]{2,1,0:T(1,128)S(1)}, u32[]{:S(2)}, u32[]{:S(2)}) %all-to-all-start) | async-done | bytes 544 | tf_op jit(solution)/shard_map/all_to_all | solution.py:125
  274.4 4.7 %all-to-all-start.1 = ((bf16[8,16,2048]{2,1,0:T(8,128)(2,1)}), bf16[8,16,2048]{2,1,0:T(8,128)(2,1)S(1)}, u32[]{:S(2)}, u32[]{:S(2)}) async-start(bf16[8,16,2048]{2,1,0:T(8,128)(2,1)} %scatter_fusion), calls=%async_computation.3 | async-start | bytes 1048576 | tf_op jit(solution)/shard_map/all_to_all | solution.py:124
  279.1 0.5 broadcast.190
  279.6 0.6 reduce.10
  280.2 0.1 reshape.159
  280.3 8.5 %all-to-all-done.1 = bf16[8,16,2048]{2,1,0:T(8,128)(2,1)S(1)} async-done(((bf16[8,16,2048]{2,1,0:T(8,128)(2,1)}), bf16[8,16,2048]{2,1,0:T(8,128)(2,1)S(1)}, u32[]{:S(2)}, u32[]{:S(2)}) %all-to-all-start.1) | async-done | bytes 524320 | tf_op jit(solution)/shard_map/all_to_all | solution.py:124
  288.8 4.6 %scatter_fusion.1 = bf16[512,2048]{1,0:T(8,128)(2,1)} fusion(bf16[512,2048]{1,0:T(8,128)(2,1)} %copy.70, s32[128]{0:T(128)S(1)} %fusion.74, bf16[128,2048]{1,0:T(8,128)(2,1)S(1)} %bitcast.61), kind=kCustom, calls=%fused_computation.2 | custom fusion | bytes 1573376 | tf_op jit(solution)/shard_map/scatter | solution.py:127
  293.4 2.3 fusion.1
  295.7 10.0 %psum.15 = f32[512]{0:T(512)S(1)} all-reduce(f32[512]{0:T(512)S(1)} %fusion.1), channel_id=1, replica_groups=mesh['section'=2,'dp'=4,'mp'=4] {'mp'}, use_global_device_ids=true, to_apply=%region_13.14 | all-reduce | flops 512 | bytes 4096 | tf_op jit(solution)/shard_map/psum | solution.py:134
  305.8 4.1 %fusion.3 = bf16[512,2048]{1,0:T(8,128)(2,1)} fusion(f32[2048]{0:T(1024)S(1)} %convert_element_type.88, f32[512]{0:T(512)S(1)} %add_rsqrt_fusion, bf16[512,2048]{1,0:T(8,128)(2,1)} %scatter_fusion.1, bf16[512,2048]{1,0:T(8,128)(2,1)} %collective-permute-done, pred[]{:T(512)S(6)} %eq.6), kind=kLoop, calls=%fused_computation.8 | loop fusion | flops 5242880 | bytes 6301697 | tf_op jit(solution)/shard_map/convert_element_type | solution.py:137
  (31 shorter events, 0.1 us)
Async XLA Ops:
  8.0 4.2 %copy-start = (bf16[1280,3,320]{0,2,1:T(8,128)(2,1)S(1)}, bf16[1280,3,320]{0,2,1:T(8,128)(2,1)}, u32[]{:S(2)}) copy-start(bf16[1280,3,320]{0,2,1:T(8,128)(2,1)} %param.19) | copy-start | bytes 7372804
  8.0 4.1 %copy-start.3 = (bf16[1280]{0:T(1024)(128)(2,1)S(1)}, bf16[1280]{0:T(1024)(128)(2,1)}, u32[]{:S(2)}) copy-start(bf16[1280]{0:T(1024)(128)(2,1)} %param.21) | copy-start | bytes 7684
  8.0 75.6 %reduce-scatter.3.cloned.1.call-start = ((), (), s32[]{:S(2)}) async-start(), calls=%async_computation.4 | async-start | bytes 3276800 | tf_op jit(solution)/shard_map/reduce_scatter | solution.py:81
  8.1 3.3 %copy-start.1 = (bf16[512,1280]{1,0:T(8,128)(2,1)S(1)}, bf16[512,1280]{1,0:T(8,128)(2,1)}, u32[]{:S(2)}) copy-start(bf16[512,1280]{1,0:T(8,128)(2,1)} %param.16) | copy-start | bytes 3932164
  14.8 4.1 %copy-start.8 = (s32[2]{0:T(128)S(1)}, s32[2]{0:T(128)}, u32[]{:S(2)}) copy-start(s32[2]{0:T(128)} %param.17) | copy-start | bytes 28
  18.9 3.4 %copy-start.2 = (bf16[2,256,1,4,80]{1,0,4,3,2:T(2,128)(2,1)S(1)}, bf16[2,256,1,4,80]{1,0,4,3,2:T(2,128)(2,1)}, u32[]{:S(2)}) copy-start(bf16[2,256,1,4,80]{1,0,4,3,2:T(2,128)(2,1)} %get-tuple-element.16) | copy-start | bytes 983044
  28.5 4.1 %copy-start.4 = (bf16[1280]{0:T(1024)(128)(2,1)S(1)}, bf16[1280]{0:T(1024)(128)(2,1)}, u32[]{:S(2)}) copy-start(bf16[1280]{0:T(1024)(128)(2,1)} %param.22) | copy-start | bytes 7684
  28.5 58.3 %all-gather.7.cloned.1.call-start = ((), (), s32[]{:S(2)}) async-start(), calls=%async_computation.6 | async-start | bytes 4915200 | tf_op jit(solution)/shard_map/all_gather | solution.py:87
  29.1 74.7 %all-gather.5.cloned.1.call-start = ((), (), s32[]{:S(2)}) async-start(), calls=%async_computation.5 | async-start | bytes 1638400 | tf_op jit(solution)/shard_map/all_gather | solution.py:92
  86.1 87.6 %all-gather.9.cloned.1.call-start = ((), (), s32[]{:S(2)}) async-start(), calls=%async_computation.8 | async-start | bytes 7864320 | tf_op jit(solution)/shard_map/all_gather | solution.py:88
  86.6 127.2 %all-reduce.2.cloned.1.call-start = ((), (), s32[]{:S(2)}) async-start(), calls=%async_computation.7 | async-start | bytes 5242880 | tf_op jit(solution)/shard_map/psum | solution.py:96
  109.5 0.7 copy-start.7
  109.6 146.7 %reduce-scatter.5.cloned.1.call-start = ((), (), s32[]{:S(2)}) async-start(), calls=%async_computation.9 | async-start | bytes 2621440 | tf_op jit(solution)/shard_map/reduce_scatter | solution.py:100
  114.8 116.5 %copy-start.9 = (s32[128]{0:T(128)S(1)}, s32[128]{0:T(128)}, u32[]{:S(2)}) copy-start(s32[128]{0:T(128)} %param.18) | copy-start | bytes 1540
  114.8 116.5 %copy-start.10 = (pred[128]{0:T(512)(128)(4,1)S(1)}, pred[128]{0:T(512)(128)(4,1)}, u32[]{:S(2)}) copy-start(pred[128]{0:T(512)(128)(4,1)} %constant.224) | copy-start | bytes 388
  114.8 122.4 %copy-start.5 = (bf16[2048]{0:T(1024)(128)(2,1)S(1)}, bf16[2048]{0:T(1024)(128)(2,1)}, u32[]{:S(2)}) copy-start(bf16[2048]{0:T(1024)(128)(2,1)} %param.26) | copy-start | bytes 12292
  225.9 53.1 %copy-start.6 = (bf16[2048]{0:T(1024)(128)(2,1)S(1)}, bf16[2048]{0:T(1024)(128)(2,1)}, u32[]{:S(2)}) copy-start(bf16[2048]{0:T(1024)(128)(2,1)} %param.29) | copy-start | bytes 12292
  225.9 67.4 %collective-permute-start = (bf16[512,2048]{1,0:T(8,128)(2,1)}, bf16[512,2048]{1,0:T(8,128)(2,1)}, u32[]{:S(2)}, u32[]{:S(2)}) collective-permute-start(bf16[512,2048]{1,0:T(8,128)(2,1)} %param.28), channel_id=1, source_target_pairs={{0,16},{1,17},{2,18},{3,19},{4,20},{5,21},{6,22},{7,23},{8,24},{9,... | collective-permute-start | bytes 6291464 | tf_op jit(solution)/shard_map/ppermute | solution.py:17
  234.0 40.4 %all-to-all-start = ((s32[8,1,16]{2,1,0:T(1,128)}), s32[8,1,16]{2,1,0:T(1,128)S(1)}, u32[]{:S(2)}, u32[]{:S(2)}) async-start(s32[8,1,16]{2,1,0:T(1,128)} %bitcast.3), calls=%async_computation | async-start | bytes 8192 | tf_op jit(solution)/shard_map/all_to_all | solution.py:125
  274.4 14.4 %all-to-all-start.1 = ((bf16[8,16,2048]{2,1,0:T(8,128)(2,1)}), bf16[8,16,2048]{2,1,0:T(8,128)(2,1)S(1)}, u32[]{:S(2)}, u32[]{:S(2)}) async-start(bf16[8,16,2048]{2,1,0:T(8,128)(2,1)} %scatter_fusion), calls=%async_computation.3 | async-start | bytes 1048576 | tf_op jit(solution)/shard_map/all_to_all | solution.py:124
Sparse Core Ops, SparseCore 0:
  28.6 54.9 reduce-scatter.2
  109.7 104.0 all-reduce.1
Sparse Core Ops, SparseCore 1:
  30.5 48.9 all-gather.6
  86.2 17.6 all-gather.4
  105.2 68.4 all-gather.8
  226.0 30.2 reduce-scatter.4
where the time goes:
time: 318 us; the launch traced here: 317 us
  waiting for transfers between devices  207 us (65%)
  matrix products  29.1 us (9%)
  local copies, waits for them, and re-layouts  24.8 us (8%)
  between operations  15.9 us (5%)
  blocking collectives  14.6 us (5%)
  starting transfers between devices  12.9 us (4%)
  other arithmetic  12.9 us (4%)
    all_gather x1, waiting for transfers between devices, per_device(): lax.all_gather(fc2_weight, 'section', axis=0, tiled=True)  58.8 us
    reduce_scatter x1, waiting for transfers between devices, per_device(): lax.psum_scatter(partial_proj.reshape(merged_rows, 4, width), 'mp', scatt...  49 us
    psum x1, waiting for transfers between devices, per_device(): first_total = lax.psum(first_partial, 'mp')  40.2 us
    reduce_scatter x1, waiting for transfers between devices, per_device(): lax.psum_scatter(jnp.dot(hidden, second_full, preferred_element_type=jnp....  19 us
    all_gather x1, waiting for transfers between devices, per_device(): lax.all_gather(merge_part, 'dp', axis=0, tiled=True)  17.1 us
    all_to_all x1, waiting for transfers between devices, per_device(): lax.all_to_all(send_place, ('section', 'dp'), split_axis=0, concat_axis=0...  13.7 us
    dot_general x1, matrix products, per_device(): jnp.dot(hidden, second_full, preferred_element_type=jnp.float32)  12.1 us
    psum x1, blocking collectives, per_device(): row_total = lax.psum(jnp.sum(entering * entering, axis=1), 'mp')  10 us
  transfers between devices with their start and end apart: 9, of which 7 were waited for; matrix products, arithmetic and copies ran while one was open for 9% of the time, Pallas kernels for 0%

commit v1 on v0

--- a/solution.py
+++ b/solution.py
@@ -22,6 +22,26 @@
     centred = centred - jnp.mean(centred, axis=-1, keepdims=True)
     variance = jnp.mean(centred * centred, axis=-1, keepdims=True)
     return centred * lax.rsqrt(variance + vit_eps) * gain.astype(jnp.float32)
+
+
+def sum_scatter_mp(blocks):
+    return lax.psum_scatter(blocks, "mp", scatter_dimension=0, tiled=False).astype(jnp.float32)
+
+
+def gather_mp(value):
+    return lax.all_gather(value, "mp", axis=0, tiled=True)
+
+
+def total_mp(value):
+    return lax.psum(value, "mp")
+
+
+def gather_groups(value):
+    return lax.all_gather(value, ("section", "dp"), axis=0, tiled=True)
+
+
+def sum_scatter_groups(value):
+    return lax.psum_scatter(value, ("section", "dp"), scatter_dimension=0, tiled=True)
 
 
 def per_device(
@@ -52,6 +72,15 @@
     group_count = section_count * lax.axis_size("dp")
     run_cap = max(2, merged_rows // group_count)
     run_total = merged_rows // run_cap
+    run_target = dest_rows.reshape(run_total, run_cap)[:, 0] // seq_rows
+    takes = jnp.arange(group_count, dtype=jnp.int32)[:, None] == run_target[None, :]
+    slot_in_tile = jnp.arange(merged_rows, dtype=jnp.int32) % (block_rows // 4)
+    tile_counts = jnp.repeat(patch_counts, block_rows // 4, total_repeat_length=merged_rows)
+    live = slot_in_tile * 4 < tile_counts
+    place = jnp.where(live, dest_rows % seq_rows - seq_rows, 0).reshape(run_total, run_cap)
+    send_place = jnp.sum(jnp.where(takes[:, :, None], place[None], 0), axis=1) + seq_rows
+    got_place = lax.all_to_all(send_place, ("section", "dp"), split_axis=0, concat_axis=0, tiled=True)
+    incoming = from_behind(section_hidden, "section", 1)
     normed_in = layer_norm(patches, attn_gain).astype(jnp.bfloat16)
     projections = jnp.dot(
         normed_in, qkv_weight.reshape(width, 3 * local_cols), preferred_element_type=jnp.float32
@@ -78,60 +107,46 @@
     own_patch = lax.dynamic_slice_in_dim(
         patches.reshape(merged_rows, 4, width), position, 1, 1
     ).reshape(merged_rows, width)
-    own_proj = lax.psum_scatter(
-        partial_proj.reshape(merged_rows, 4, width), "mp", scatter_dimension=1, tiled=True
-    ).reshape(merged_rows, width)
+    own_proj = sum_scatter_mp(
+        partial_proj.astype(jnp.bfloat16).reshape(merged_rows, 4, width).transpose(1, 0, 2)
+    )
     block_out = (own_patch.astype(jnp.float32) + own_proj).astype(jnp.bfloat16)
     merge_part = layer_norm(block_out, merge_gain).astype(jnp.bfloat16)
-    first_full, second_full, bias_full = (
-        lax.all_gather(fc1_weight, "section", axis=1, tiled=True),
-        lax.all_gather(fc2_weight, "section", axis=0, tiled=True),
-        lax.all_gather(fc1_bias, "section", axis=0, tiled=True),
+    lane_same = jnp.arange(run_cap)[:, None] == jnp.arange(run_cap)[None, :]
+    order = (takes[:, None, :, None] & lane_same[None, :, None, :]).reshape(
+        group_count * run_cap, merged_rows
     )
-    first_partial = jnp.dot(
-        lax.all_gather(merge_part, "dp", axis=0, tiled=True),
-        first_full,
-        preferred_element_type=jnp.float32,
+    merge_part = jnp.dot(
+        order.astype(jnp.bfloat16), merge_part, preferred_element_type=jnp.float32
+    ).astype(jnp.bfloat16)
+    slot_rows = group_count * run_cap
+    gathered = gather_groups(merge_part)
+    gathered = (
+        gathered.reshape(group_count, group_count, run_cap, width)
+        .transpose(1, 0, 2, 3)
+        .reshape(group_count * slot_rows, width)
     )
-    first_total = lax.psum(first_partial, "mp")
-    hidden = jax.nn.gelu(first_total + bias_full.astype(jnp.float32), approximate=False).astype(
-        jnp.bfloat16
+    first_partial = jnp.dot(gathered, fc1_weight, preferred_element_type=jnp.float32)
+    mp_count = lax.axis_size("mp")
+    first_total = sum_scatter_mp(
+        first_partial.astype(jnp.bfloat16).reshape(mp_count, -1, fc1_weight.shape[1])
     )
-    embed_total = lax.psum_scatter(
-        jnp.dot(hidden, second_full, preferred_element_type=jnp.float32).astype(jnp.bfloat16),
-        "dp",
-        scatter_dimension=0,
-        tiled=True,
-    ).astype(jnp.float32)
+    hidden_part = jax.nn.gelu(
+        first_total + fc1_bias.astype(jnp.float32), approximate=False
+    ).astype(jnp.bfloat16)
+    hidden = gather_mp(hidden_part)
+    second_partial = jnp.dot(hidden, fc2_weight, preferred_element_type=jnp.float32)
+    embed_total = sum_scatter_groups(second_partial.astype(jnp.bfloat16)).astype(jnp.float32)
     image_embeds = (embed_total + fc2_bias.astype(jnp.float32)).astype(jnp.bfloat16)
-    slot_in_tile = jnp.arange(merged_rows, dtype=jnp.int32) % (block_rows // 4)
-    tile_counts = jnp.repeat(patch_counts, block_rows // 4, total_repeat_length=merged_rows)
-    live = slot_in_tile * 4 < tile_counts
-    receiver = dest_rows // seq_rows
-    run_target = receiver.reshape(run_total, run_cap)[:, 0]
-    place = jnp.where(live, dest_rows % seq_rows, seq_rows)
-    send_rows = (
-        jnp.zeros((group_count, run_cap, feature_cols), jnp.bfloat16)
-        .at[run_target]
-        .set(image_embeds.reshape(run_total, run_cap, feature_cols))
-    )
-    send_place = (
-        jnp.full((group_count, run_cap), seq_rows, jnp.int32)
-        .at[run_target]
-        .set(place.reshape(run_total, run_cap))
-    )
-    got_rows, got_place = (
-        lax.all_to_all(send_rows, ("section", "dp"), split_axis=0, concat_axis=0, tiled=True),
-        lax.all_to_all(send_place, ("section", "dp"), split_axis=0, concat_axis=0, tiled=True),
-    )
-    sequence_embeds = text_embeds.at[got_place.reshape(-1)].set(
-        got_rows.reshape(-1, feature_cols), mode="drop"
-    )
-    incoming = from_behind(section_hidden, "section", 1)
+    hits = got_place.reshape(1, -1) == jnp.arange(seq_rows, dtype=jnp.int32)[:, None]
+    placed = jnp.dot(
+        hits.astype(jnp.bfloat16), image_embeds, preferred_element_type=jnp.float32
+    ).astype(jnp.bfloat16)
+    sequence_embeds = jnp.where(jnp.any(hits, axis=1)[:, None], placed, text_embeds)
     entering = jnp.where(lax.axis_index("section") == 0, sequence_embeds, incoming).astype(
         jnp.float32
     )
-    row_total = lax.psum(jnp.sum(entering * entering, axis=1), "mp")
+    row_total = total_mp(jnp.sum(entering * entering, axis=1))
     layer_inputs = (
         entering * lax.rsqrt(row_total / HID + llm_eps)[:, None] * llm_gain.astype(jnp.float32)
     ).astype(jnp.bfloat16)

time: 318 us -> 271 us (0.85)
  waiting for transfers between devices: 207 us -> 174 us
  local copies, waits for them, and re-layouts: 24.8 us -> 19.9 us
  starting transfers between devices: 12.9 us -> 8.56 us
  other arithmetic: 12.9 us -> 16.9 us
  blocking collectives: 14.6 us -> 10.7 us
    all_to_all x1, waiting for transfers between devices: 13.7 us -> 54 us  [per_device(): lax.all_to_all(send_place, ('section', 'dp'), split_axis=0, concat_axis=0...]
    psum x1 -> x0, waiting for transfers between devices: 40.2 us -> none  [per_device(): first_total = lax.psum(first_partial, 'mp')]
    all_gather x3 -> x2, waiting for transfers between devices: 75.9 us -> 60.1 us  [the longest x1 31.3 us: gather_mp(): return lax.all_gather(value, 'mp', axis=0, tiled=True)]
    reduce_scatter x2 -> x3, waiting for transfers between devices: 68 us -> 59.4 us  [the longest x2 59.4 us: sum_scatter_mp(): lax.psum_scatter(blocks, 'mp', scatter_dimension=0, tiled=False)]
    all_to_all x1 -> x0, waiting for transfers between devices: 8.45 us -> none  [per_device(): lax.all_to_all(send_rows, ('section', 'dp'), split_axis=0, concat_axis=0,...]
    scatter x3 -> x0, local copies, waits for them, and re-layouts: 8.22 us -> none  [the longest x1 4.61 us: per_device(): text_embeds.at[got_place.reshape(-1)]]
    reshape x3 -> x4, local copies, waits for them, and re-layouts: 0.23 us -> 8.14 us  [the longest x2 5.99 us: per_device(): partial_proj.astype(jnp.bfloat16).reshape(merged_rows, 4, width)]
    all_to_all x1 -> x0, starting transfers between devices: 4.66 us -> none  [per_device(): lax.all_to_all(send_rows, ('section', 'dp'), split_axis=0, concat_axis=0,...]
  transfers between devices with their start and end apart: 9 -> 7, of which waited for: 7 -> 5; matrix products, arithmetic and copies ran while one was open for 9% -> 4% of each run, Pallas kernels for 0% -> 0%
where the time goes in v1:
time: 271 us; the launch traced here: 270 us
  waiting for transfers between devices  174 us (64%)
  matrix products  26.2 us (10%)
  local copies, waits for them, and re-layouts  19.9 us (7%)
  other arithmetic  16.9 us (6%)
  between operations  14 us (5%)
  blocking collectives  10.7 us (4%)
  starting transfers between devices  8.56 us (3%)
    reduce_scatter x2, waiting for transfers between devices, sum_scatter_mp(): lax.psum_scatter(blocks, 'mp', scatter_dimension=0, tiled=False)  59.4 us
    all_to_all x1, waiting for transfers between devices, per_device(): lax.all_to_all(send_place, ('section', 'dp'), split_axis=0, concat_axis=0...  54 us
    all_gather x1, waiting for transfers between devices, gather_mp(): return lax.all_gather(value, 'mp', axis=0, tiled=True)  31.3 us
    all_gather x1, waiting for transfers between devices, gather_groups(): return lax.all_gather(value, ('section', 'dp'), axis=0, tiled=True)  28.8 us
    psum x1, blocking collectives, total_mp(): return lax.psum(value, 'mp')  10.7 us
    dot_general x1, matrix products, per_device(): jnp.dot(hidden, fc2_weight, preferred_element_type=jnp.float32)  6.27 us
    reshape x2, local copies, waits for them, and re-layouts, per_device(): partial_proj.astype(jnp.bfloat16).reshape(merged_rows, 4, width)  5.99 us
  transfers between devices with their start and end apart: 7, of which 5 were waited for; matrix products, arithmetic and copies ran while one was open for 4% of the time, Pallas kernels for 0%

profile of v1, /device:TPU:0, one launch (start us, length us, event | category | flops | bytes accessed | tf_op | source)
XLA Modules:
  0.0 269.8 jit_solution(1609884030651612214)
XLA Ops:
  7.2 0.0 copy-start
  7.2 0.0 copy-start.3
  7.2 0.0 reduce-scatter.4.cloned.1.call-start
  7.2 0.0 copy-start.1
  7.2 1.7 convert_reduce_fusion
  9.0 0.1 copy-done.1
  9.1 0.5 fusion.7
  9.6 4.3 %convolution_convert_fusion.5 = bf16[512,960]{0,1:T(8,128)(2,1)} fusion(bf16[1280,960]{0,1:T(8,128)(2,1)} %bitcast.95, bf16[512,1280]{1,0:T(8,128)(2,1)S(1)} %copy-done.1, f32[1280]{0:T(1024)S(1)} %convert_element_type.118, f32[512]{0:T(512)S(1)} %add_rsqrt_fusion.1, f32[512]{0:T(512)S(1)} %broadcast_multiply_fusion), kind=kOutput, calls=%fused_computation.24 | convolution fusion | flops 1262059520 | bytes 4760576 | tf_op jit(solution)/shard_map/dot_general | solution.py:85
  13.9 3.3 %reshape.265 = bf16[2,256,3,4,80]{1,0,4,3,2:T(2,128)(2,1)} reshape(bf16[512,960]{0,1:T(8,128)(2,1)} %convolution_convert_fusion.5) | data formatting | bytes 1966080 | tf_op jit(solution)/shard_map/reshape | solution.py:88
  17.2 2.7 %fusion.71 = (bf16[2,256,1,4,80]{1,0,4,3,2:T(2,128)(2,1)S(1)}, bf16[2,256,1,4,80]{1,0,4,3,2:T(2,128)(2,1)S(1)}, bf16[2,256,1,4,80]{1,0,4,3,2:T(2,128)(2,1)}) fusion(bf16[2,256,3,4,80]{1,0,4,3,2:T(2,128)(2,1)} %reshape.265), kind=kLoop, calls=%fused_computation.118 | loop fusion | bytes 1966080 | tf_op jit(solution)/shard_map/slice | solution.py:91
  19.9 0.1 iota_compare_fusion.4
  19.9 3.2 %fusion.73 = (f32[2,4,256]{2,1,0:T(4,128)S(1)}, f32[2,4,256,256]{2,3,1,0:T(8,128)}) fusion(pred[2,256]{1,0:T(4,128)(4,1)S(1)} %iota_compare_fusion.4, bf16[2,256,1,4,80]{1,0,4,3,2:T(2,128)(2,1)} %get-tuple-element.16, bf16[2,256,1,4,80]{1,0,4,3,2:T(2,128)(2,1)S(1)} %get-tuple-element.15), kind=kOutput, calls=%fused_computation.120 | convolution fusion | flops 85983488 | bytes 2761216 | tf_op jit(solution)/shard_map/sub | solution.py:100
  23.1 2.0 fusion.15
  25.1 0.3 copy.50
  25.5 1.9 convolution_convert_fusion.2
  27.4 3.5 %reshape.267 = bf16[128,4,1280]{2,1,0:T(4,128)(2,1)} reshape(bf16[512,1280]{1,0:T(8,128)(2,1)} %convolution_convert_fusion.2) | data formatting | bytes 2621440 | tf_op jit(solution)/shard_map/reshape | solution.py:111
  30.9 2.5 copy.92
  33.4 0.0 reduce-scatter.4.cloned.1.call-update
  33.4 0.0 all-gather.3.cloned.1.call-start
  33.5 3.5 %reshape.263 = bf16[128,4,1280]{2,1,0:T(4,128)(2,1)} reshape(bf16[512,1280]{1,0:T(8,128)(2,1)} %param.16) | data formatting | bytes 2621440 | tf_op jit(solution)/shard_map/reshape | solution.py:108
  37.0 0.0 copy-done.8
  37.0 0.1 reshape.262
  37.1 0.1 slice_reduce_fusion
  37.2 0.1 broadcast_and_fusion
  37.4 0.2 and.61
  37.6 0.0 copy-done.4
  37.6 1.9 dynamic-slice_convert_fusion
  39.5 28.1 %reduce-scatter.4.cloned.1.call-done = bf16[1,128,1280]{2,1,0:T(8,128)(2,1)} async-done(((bf16[4,128,1280]{2,1,0:T(8,128)(2,1)}), bf16[1,128,1280]{2,1,0:T(8,128)(2,1)}) %reduce-scatter.4.cloned.1.call-update) | async-done | bytes 327696 | tf_op jit(solution)/shard_map/reduce_scatter | solution.py:28
  67.7 1.2 convert_reduce_fusion.1
  68.9 1.2 fusion.20
  70.1 1.1 convolution_convert_fusion.3
  71.2 0.0 all-gather.3.cloned.1.call-update
  71.2 0.0 reduce-scatter.6.cloned.1.call-start
  71.2 28.8 %all-gather.3.cloned.1.call-done = bf16[1024,1280]{1,0:T(8,128)(2,1)} async-done(((bf16[128,1280]{1,0:T(8,128)(2,1)}), bf16[1024,1280]{1,0:T(8,128)(2,1)}) %all-gather.3.cloned.1.call-update) | async-done | bytes 2621456 | tf_op jit(solution)/shard_map/all_gather | solution.py:40
  100.0 2.1 copy.53
  102.1 0.1 copy-done.11
  102.2 3.3 %convolution_convert_fusion.4 = bf16[1024,640]{1,0:T(8,128)(2,1)} fusion(bf16[1024,1280]{1,0:T(8,128)(2,1)S(1)} %bitcast.91, bf16[1280,640]{1,0:T(8,128)(2,1)S(1)} %copy-done.11), kind=kOutput, calls=%fused_computation.23 | convolution fusion | flops 1678376960 | bytes 5570560 | tf_op jit(solution)/shard_map/dot_general | solution.py:129
  105.5 0.0 reduce-scatter.6.cloned.1.call-update
  105.5 0.2 all-gather.5.cloned.1.call-start
  105.7 0.0 copy-done.7
  105.8 31.3 %reduce-scatter.6.cloned.1.call-done = bf16[1,256,640]{2,1,0:T(8,128)(2,1)} async-done(((bf16[4,256,640]{2,1,0:T(8,128)(2,1)}), bf16[1,256,640]{2,1,0:T(8,128)(2,1)}) %reduce-scatter.6.cloned.1.call-update) | async-done | bytes 327696 | tf_op jit(solution)/shard_map/reduce_scatter | solution.py:28
  137.0 3.2 %fusion.27 = bf16[256,640]{1,0:T(8,128)(2,1)} fusion(bf16[1,256,640]{2,1,0:T(8,128)(2,1)} %reduce-scatter.6.cloned.1.call-done, f32[640]{0:T(1024)S(1)} %convert_element_type.142), kind=kLoop, calls=%fused_computation.48 | loop fusion | flops 10977280 | bytes 657920 | tf_op jit(solution)/shard_map/convert_element_type | solution.py:136
  140.2 0.0 all-gather.5.cloned.1.call-update
  140.2 0.0 reduce-scatter.8.cloned.1.call-start
  140.2 31.3 %all-gather.5.cloned.1.call-done = bf16[1024,640]{1,0:T(8,128)(2,1)} async-done(((bf16[256,640]{1,0:T(8,128)(2,1)}), bf16[1024,640]{1,0:T(8,128)(2,1)}) %all-gather.5.cloned.1.call-update) | async-done | bytes 1310736 | tf_op jit(solution)/shard_map/all_gather | solution.py:32
  171.5 6.3 %convolution_convert_fusion = bf16[1024,2048]{1,0:T(8,128)(2,1)} fusion(bf16[1024,640]{1,0:T(8,128)(2,1)} %all-gather.5.cloned.1.call-done, bf16[640,2048]{1,0:T(8,128)(2,1)S(1)} %copy-done), kind=kOutput, calls=%fused_computation.6 | convolution fusion | flops 2686451712 | bytes 8126464 | tf_op jit(solution)/shard_map/dot_general | solution.py:138
  177.8 0.0 reduce-scatter.8.cloned.1.call-update
  177.8 4.9 %collective-permute-start = (bf16[512,2048]{1,0:T(8,128)(2,1)}, bf16[512,2048]{1,0:T(8,128)(2,1)}, u32[]{:S(2)}, u32[]{:S(2)}) collective-permute-start(bf16[512,2048]{1,0:T(8,128)(2,1)} %param.28), channel_id=1, source_target_pairs={{0,16},{1,17},{2,18},{3,19},{4,20},{5,21},{6,22},{7,23},{8,24},{9,... | collective-permute-start | bytes 6291464 | tf_op jit(solution)/shard_map/ppermute | solution.py:17
  182.7 0.6 fusion.72
  183.3 1.3 compare_select_fusion.2
  184.6 0.1 broadcast_in_dim.46
  184.7 0.1 select_reduce_fusion
  184.8 0.6 broadcast_add_fusion
  185.4 3.3 %all-to-all-start = ((s32[8,1,16]{2,1,0:T(1,128)}), s32[8,1,16]{2,1,0:T(1,128)S(1)}, u32[]{:S(2)}, u32[]{:S(2)}) async-start(s32[8,1,16]{2,1,0:T(1,128)} %bitcast.3), calls=%async_computation | async-start | bytes 8192 | tf_op jit(solution)/shard_map/all_to_all | solution.py:82
  188.7 54.0 %all-to-all-done = s32[8,1,16]{2,1,0:T(1,128)S(1)} async-done(((s32[8,1,16]{2,1,0:T(1,128)}), s32[8,1,16]{2,1,0:T(1,128)S(1)}, u32[]{:S(2)}, u32[]{:S(2)}) %all-to-all-start) | async-done | bytes 544 | tf_op jit(solution)/shard_map/all_to_all | solution.py:82
  242.7 0.5 broadcast.236
  243.2 0.7 reduce.7
  243.9 0.1 eq.62
  244.0 0.2 fusion.64
  244.1 0.0 collective-permute-done
  244.1 0.0 reduce-scatter.8.cloned.1.call-done
  244.2 4.3 %fusion.1 = (f32[512]{0:T(512)S(1)}, bf16[512,2048]{1,0:T(8,128)(2,1)}) fusion(bf16[512,2048]{1,0:T(8,128)(2,1)} %collective-permute-done, pred[]{:T(512)S(6)} %eq.69, bf16[512,2048]{1,0:T(8,128)(2,1)} %param.27, bf16[128,2048]{1,0:T(8,128)(2,1)} %reduce-scatter.8.cloned.1.call-done, f32[2048]{0:T(1024)S(1)} %convert_element_type.146, s32[128]{0:T(128)S(1)} %eq.62, ...), kind=kOutput, calls=%fused_computation.3 | convolution fusion | flops 275578368 | bytes 6827009 | tf_op jit(solution)/shard_map/dot_general | solution.py:142
  248.4 10.7 %psum.7 = f32[512]{0:T(512)S(1)} all-reduce(f32[512]{0:T(512)S(1)} %get-tuple-element.21), channel_id=1, replica_groups=mesh['section'=2,'dp'=4,'mp'=4] {'mp'}, use_global_device_ids=true, to_apply=%region_12.13 | all-reduce | flops 512 | bytes 4096 | tf_op jit(solution)/shard_map/psum | solution.py:36
  259.1 4.1 %fusion.3 = bf16[512,2048]{1,0:T(8,128)(2,1)} fusion(f32[2048]{0:T(1024)S(1)} %convert_element_type.150, f32[512]{0:T(512)S(1)} %add_rsqrt_fusion, bf16[512,2048]{1,0:T(8,128)(2,1)} %get-tuple-element.22, bf16[512,2048]{1,0:T(8,128)(2,1)} %collective-permute-done, pred[]{:T(512)S(6)} %eq.69), kind=kLoop, calls=%fused_computation.5 | loop fusion | flops 5242880 | bytes 6301697 | tf_op jit(solution)/shard_map/convert_element_type | solution.py:152
  (32 shorter events, 0.2 us)
Async XLA Ops:
  7.2 164.4 %copy-start = (bf16[640,2048]{1,0:T(8,128)(2,1)S(1)}, bf16[640,2048]{1,0:T(8,128)(2,1)}, u32[]{:S(2)}) copy-start(bf16[640,2048]{1,0:T(8,128)(2,1)} %param.25) | copy-start | bytes 7864324
  7.2 2.4 copy-start.3
  7.2 60.5 %reduce-scatter.4.cloned.1.call-start = ((), (), s32[]{:S(2)}) async-start(), calls=%async_computation.4 | async-start | bytes 1638400 | tf_op jit(solution)/shard_map/reduce_scatter | solution.py:28
  7.2 1.9 copy-start.1
  13.9 6.0 %copy-start.9 = (s32[2]{0:T(128)S(1)}, s32[2]{0:T(128)}, u32[]{:S(2)}) copy-start(s32[2]{0:T(128)} %param.17) | copy-start | bytes 28
  23.1 2.4 copy-start.12
  33.4 3.6 %copy-start.8 = (s32[128]{0:T(128)S(1)}, s32[128]{0:T(128)}, u32[]{:S(2)}) copy-start(s32[128]{0:T(128)} %param.18) | copy-start | bytes 1540
  33.4 4.2 %copy-start.4 = (bf16[1280]{0:T(1024)(128)(2,1)S(1)}, bf16[1280]{0:T(1024)(128)(2,1)}, u32[]{:S(2)}) copy-start(bf16[1280]{0:T(1024)(128)(2,1)} %param.22) | copy-start | bytes 7684
  33.4 66.6 %all-gather.3.cloned.1.call-start = ((), (), s32[]{:S(2)}) async-start(), calls=%async_computation.5 | async-start | bytes 2949120 | tf_op jit(solution)/shard_map/all_gather | solution.py:40
  67.7 2.4 copy-start.2
  71.2 65.8 %reduce-scatter.6.cloned.1.call-start = ((), (), s32[]{:S(2)}) async-start(), calls=%async_computation.6 | async-start | bytes 1638400 | tf_op jit(solution)/shard_map/reduce_scatter | solution.py:28
  100.0 2.2 copy-start.11
  102.2 3.5 %copy-start.7 = (bf16[640]{0:T(1024)(128)(2,1)S(1)}, bf16[640]{0:T(1024)(128)(2,1)}, u32[]{:S(2)}) copy-start(bf16[640]{0:T(1024)(128)(2,1)} %param.24) | copy-start | bytes 3844
  105.5 66.0 %all-gather.5.cloned.1.call-start = ((), (), s32[]{:S(2)}) async-start(), calls=%async_computation.7 | async-start | bytes 1638400 | tf_op jit(solution)/shard_map/all_gather | solution.py:32
  140.2 104.0 %reduce-scatter.8.cloned.1.call-start = ((), (), s32[]{:S(2)}) async-start(), calls=%async_computation.8 | async-start | bytes 4718592 | tf_op jit(solution)/shard_map/reduce_scatter | solution.py:44
  177.8 5.5 %copy-start.10 = (pred[128]{0:T(512)(128)(4,1)S(1)}, pred[128]{0:T(512)(128)(4,1)}, u32[]{:S(2)}) copy-start(pred[128]{0:T(512)(128)(4,1)} %constant.223) | copy-start | bytes 388
  177.8 10.9 %copy-start.5 = (bf16[2048]{0:T(1024)(128)(2,1)S(1)}, bf16[2048]{0:T(1024)(128)(2,1)}, u32[]{:S(2)}) copy-start(bf16[2048]{0:T(1024)(128)(2,1)} %param.26) | copy-start | bytes 12292
  177.8 10.9 %copy-start.6 = (bf16[2048]{0:T(1024)(128)(2,1)S(1)}, bf16[2048]{0:T(1024)(128)(2,1)}, u32[]{:S(2)}) copy-start(bf16[2048]{0:T(1024)(128)(2,1)} %param.29) | copy-start | bytes 12292
  177.8 66.3 %collective-permute-start = (bf16[512,2048]{1,0:T(8,128)(2,1)}, bf16[512,2048]{1,0:T(8,128)(2,1)}, u32[]{:S(2)}, u32[]{:S(2)}) collective-permute-start(bf16[512,2048]{1,0:T(8,128)(2,1)} %param.28), channel_id=1, source_target_pairs={{0,16},{1,17},{2,18},{3,19},{4,20},{5,21},{6,22},{7,23},{8,24},{9,... | collective-permute-start | bytes 6291464 | tf_op jit(solution)/shard_map/ppermute | solution.py:17
  185.4 57.4 %all-to-all-start = ((s32[8,1,16]{2,1,0:T(1,128)}), s32[8,1,16]{2,1,0:T(1,128)S(1)}, u32[]{:S(2)}, u32[]{:S(2)}) async-start(s32[8,1,16]{2,1,0:T(1,128)} %bitcast.3), calls=%async_computation | async-start | bytes 8192 | tf_op jit(solution)/shard_map/all_to_all | solution.py:82
Sparse Core Ops, SparseCore 0:
  33.6 34.0 reduce-scatter.3
  71.3 28.6 all-gather.2
  105.6 31.3 reduce-scatter.5
  140.3 31.1 all-gather.4
  178.0 63.4 reduce-scatter.7

commit v2 on v1

--- a/solution.py
+++ b/solution.py
@@ -1,6 +1,11 @@
+import functools
+import math
+
 import jax
 import jax.numpy as jnp
 from jax import lax
+from jax.experimental import pallas as pl
+from jax.experimental.pallas import tpu as pltpu
 from jax.sharding import PartitionSpec as P
 
 HEAD_DIM = 80
@@ -24,24 +29,269 @@
     return centred * lax.rsqrt(variance + vit_eps) * gain.astype(jnp.float32)
 
 
-def sum_scatter_mp(blocks):
-    return lax.psum_scatter(blocks, "mp", scatter_dimension=0, tiled=False).astype(jnp.float32)
+VMEM_LIMIT = 60 * 1024 * 1024
+KERNEL_BYTES = 8 * 1024 * 1024
+
+
+def vmem_call(kernel, out, scratch, sent_bytes, ident, *operands):
+    return pl.pallas_call(
+        kernel,
+        out_shape=out,
+        in_specs=[pl.BlockSpec(memory_space=pltpu.VMEM)] * len(operands),
+        out_specs=pl.BlockSpec(memory_space=pltpu.VMEM),
+        scratch_shapes=scratch,
+        cost_estimate=pl.CostEstimate(
+            flops=sent_bytes * 20000, bytes_accessed=sent_bytes * 2, transcendentals=0
+        ),
+        compiler_params=pltpu.CompilerParams(
+            collective_id=ident, has_side_effects=True, vmem_limit_bytes=VMEM_LIMIT
+        ),
+    )(*operands)
+
+
+def exchange_kernel(count, spread, x_ref, o_ref, send_sem, recv_sem, own_sem):
+    me = lax.axis_index("mp")
+    barrier = pltpu.get_barrier_semaphore()
+    for step in range(1, count):
+        peer = lax.rem(me + step, count)
+        pl.semaphore_signal(
+            barrier, inc=1, device_id={"mp": peer}, device_id_type=pl.DeviceIdType.MESH
+        )
+    pl.semaphore_wait(barrier, count - 1)
+    copies = []
+    for step in sorted(range(1, count), key=lambda s: -min(s, count - s)):
+        peer = lax.rem(me + step, count)
+        copy = pltpu.make_async_remote_copy(
+            src_ref=x_ref.at[peer] if spread else x_ref,
+            dst_ref=o_ref.at[me],
+            send_sem=send_sem.at[step - 1],
+            recv_sem=recv_sem.at[step - 1],
+            device_id={"mp": peer},
+            device_id_type=pl.DeviceIdType.MESH,
+        )
+        copy.start()
+        copies.append(copy)
+    own = pltpu.make_async_copy(x_ref.at[me] if spread else x_ref, o_ref.at[me], own_sem)
+    own.start()
+    own.wait()
+    for copy in copies:
+        copy.wait()
+
+
+def exchange_mp(value, spread, ident):
+    count = lax.axis_size("mp")
+    shape = value.shape if spread else (count,) + value.shape
+    size = math.prod(shape) * value.dtype.itemsize
+    return vmem_call(
+        functools.partial(exchange_kernel, count, spread),
+        jax.ShapeDtypeStruct(shape, value.dtype),
+        [
+            pltpu.SemaphoreType.DMA((count - 1,)),
+            pltpu.SemaphoreType.DMA((count - 1,)),
+            pltpu.SemaphoreType.DMA,
+        ],
+        size,
+        ident,
+        value,
+    )
+
+
+def sum_scatter_mp(blocks, ident):
+    return jnp.sum(exchange_mp(blocks, True, ident).astype(jnp.float32), axis=0)
 
 
 def gather_mp(value):
-    return lax.all_gather(value, "mp", axis=0, tiled=True)
+    got = exchange_mp(value, False, 2)
+    return got.reshape((-1,) + value.shape[1:])
 
 
 def total_mp(value):
-    return lax.psum(value, "mp")
+    return jnp.sum(exchange_mp(value.reshape(-1, 128), False, 3), axis=0).reshape(-1)
+
+
+def flip(index, bit):
+    return index + bit * (1 - 2 * (index // bit % 2))
+
+
+def group_bits():
+    outer = [("dp", 1 << k) for k in range(1, lax.axis_size("dp").bit_length() - 1)]
+    outer += [("section", 1 << k) for k in range(lax.axis_size("section").bit_length() - 1)]
+    return outer, ("dp", 1)
+
+
+def meets(axis, bit):
+    return {axis: flip(lax.axis_index(axis), bit)}
+
+
+def group_at(mask):
+    spots = {axis: lax.axis_index(axis) for axis in ("section", "dp")}
+    for axis, bit in mask:
+        spots[axis] = flip(spots[axis], bit)
+    return spots["section"] * lax.axis_size("dp") + spots["dp"]
+
+
+def greet(bits):
+    barrier = pltpu.get_barrier_semaphore()
+    for axis, bit in bits:
+        pl.semaphore_signal(
+            barrier, inc=1, device_id=meets(axis, bit), device_id_type=pl.DeviceIdType.MESH
+        )
+    pl.semaphore_wait(barrier, len(bits))
+
+
+def gather_kernel(x_ref, o_ref, send_sem, recv_sem, own_sem):
+    outer, last = group_bits()
+    greet(outer + [last])
+    half = x_ref.shape[1] // 2
+    sent, waiting = [], []
+    slots = iter(range(send_sem.shape[0]))
+
+    def pass_on(mask, stage, part, order):
+        cols = pl.ds(part * half, half)
+        spot = group_at(mask)
+        source = o_ref.at[spot, :, cols] if mask else x_ref.at[:, cols]
+        for later in range(stage, len(order)):
+            slot = next(slots)
+            copy = pltpu.make_async_remote_copy(
+                src_ref=source,
+                dst_ref=o_ref.at[spot, :, cols],
+                send_sem=send_sem.at[slot],
+                recv_sem=recv_sem.at[slot],
+                device_id=meets(*order[later]),
+                device_id_type=pl.DeviceIdType.MESH,
+            )
+            copy.start()
+            sent.append(copy)
+            waiting.append((later, copy, mask + [order[later]], part, order))
+
+    pass_on([], 0, 0, outer + [last])
+    pass_on([], 0, 1, outer[::-1] + [last])
+    own = pltpu.make_async_copy(x_ref, o_ref.at[group_at([])], own_sem)
+    own.start()
+    while waiting:
+        first = min(range(len(waiting)), key=lambda at: waiting[at][0])
+        stage, copy, mask, part, order = waiting.pop(first)
+        copy.wait_recv()
+        pass_on(mask, stage + 1, part, order)
+    for copy in sent:
+        copy.wait_send()
+    own.wait()
 
 
 def gather_groups(value):
-    return lax.all_gather(value, ("section", "dp"), axis=0, tiled=True)
+    count = lax.axis_size("section") * lax.axis_size("dp")
+    size = count * value.size * value.dtype.itemsize
+    if size > KERNEL_BYTES:
+        return lax.all_gather(value, ("section", "dp"), axis=0, tiled=True)
+    slots = 2 * (count - 1)
+    got = vmem_call(
+        gather_kernel,
+        jax.ShapeDtypeStruct((count,) + value.shape, value.dtype),
+        [
+            pltpu.SemaphoreType.DMA((slots,)),
+            pltpu.SemaphoreType.DMA((slots,)),
+            pltpu.SemaphoreType.DMA,
+        ],
+        size,
+        4,
+        value,
+    )
+    return got.reshape(-1, value.shape[1])
+
+
+def scatter_kernel(x_ref, o_ref, held, taken, send_sem, recv_sem):
+    outer, first = group_bits()
+    greet(outer + [first])
+    rows = x_ref.shape[1]
+    half = x_ref.shape[2] // 2
+    chunk = 32
+    orders = ([first] + outer, [first] + outer[::-1])
+    slots = iter(range(send_sem.shape[0]))
+    masks = [[]]
+    for bit in outer:
+        masks = masks + [mask + [bit] for mask in masks]
+    place_of = {frozenset(mask): at for at, mask in enumerate(masks)}
+    base = len(masks)
+    live = {}
+
+    def send(part, stage):
+        cols = pl.ds(part * half, half)
+        bit = orders[part][stage]
+        kept = orders[part][stage + 1 :]
+        copies = []
+        for mask in [m for m in masks if set(m) <= set(kept)]:
+            if stage == 0:
+                source = x_ref.at[group_at(mask + [bit]), :, cols]
+            else:
+                source = held.at[place_of[frozenset(mask + [bit])], :, cols]
+            landing = 2 * base - 2 ** (len(kept) + 1) + [
+                m for m in masks if set(m) <= set(kept)
+            ].index(mask)
+            slot = next(slots)
+            copy = pltpu.make_async_remote_copy(
+                src_ref=source,
+                dst_ref=taken.at[landing, :, cols],
+                send_sem=send_sem.at[slot],
+                recv_sem=recv_sem.at[slot],
+                device_id=meets(*bit),
+                device_id_type=pl.DeviceIdType.MESH,
+            )
+            copy.start()
+            copies.append((copy, mask, landing))
+        live[part, stage] = copies
+
+    def add(part, stage):
+        cols = pl.ds(part * half, half)
+        final = stage + 1 == len(orders[part])
+        following = None if final else orders[part][stage + 1]
+        copies = live[part, stage]
+        for copy, mask, landing in sorted(copies, key=lambda c: following not in c[1]):
+            copy.wait_recv()
+            at = place_of[frozenset(mask)]
+            spot = group_at(mask)
+
+            @pl.loop(0, rows // chunk)
+            def _(step):
+                span = pl.ds(step * chunk, chunk)
+                mine = x_ref[spot, span, cols] if stage == 0 else held[at, span, cols]
+                total = mine.astype(jnp.float32) + taken[landing, span, cols].astype(jnp.float32)
+                if final:
+                    o_ref[span, cols] = total
+                else:
+                    held[at, span, cols] = total.astype(held.dtype)
+
+    send(0, 0)
+    send(1, 0)
+    for stage in range(len(orders[0])):
+        for part in (0, 1):
+            add(part, stage)
+            if stage + 1 < len(orders[0]):
+                send(part, stage + 1)
+    for copies in live.values():
+        for copy, _, _ in copies:
+            copy.wait_send()
 
 
 def sum_scatter_groups(value):
-    return lax.psum_scatter(value, ("section", "dp"), scatter_dimension=0, tiled=True)
+    count = lax.axis_size("section") * lax.axis_size("dp")
+    size = value.size * value.dtype.itemsize
+    if size > KERNEL_BYTES:
+        return lax.psum_scatter(value, ("section", "dp"), scatter_dimension=0, tiled=True)
+    rows, cols = value.shape[0] // count, value.shape[1]
+    slots = 2 * (count - 1)
+    return vmem_call(
+        scatter_kernel,
+        jax.ShapeDtypeStruct((rows, cols), jnp.float32),
+        [
+            pltpu.VMEM((count // 2, rows, cols), value.dtype),
+            pltpu.VMEM((count - 1, rows, cols), value.dtype),
+            pltpu.SemaphoreType.DMA((slots,)),
+            pltpu.SemaphoreType.DMA((slots,)),
+        ],
+        size,
+        5,
+        value.reshape(count, rows, cols),
+    )
 
 
 def per_device(
@@ -108,7 +358,8 @@
         patches.reshape(merged_rows, 4, width), position, 1, 1
     ).reshape(merged_rows, width)
     own_proj = sum_scatter_mp(
-        partial_proj.astype(jnp.bfloat16).reshape(merged_rows, 4, width).transpose(1, 0, 2)
+        partial_proj.astype(jnp.bfloat16).reshape(merged_rows, 4, width).transpose(1, 0, 2),
+        0,
     )
     block_out = (own_patch.astype(jnp.float32) + own_proj).astype(jnp.bfloat16)
     merge_part = layer_norm(block_out, merge_gain).astype(jnp.bfloat16)
@@ -129,7 +380,8 @@
     first_partial = jnp.dot(gathered, fc1_weight, preferred_element_type=jnp.float32)
     mp_count = lax.axis_size("mp")
     first_total = sum_scatter_mp(
-        first_partial.astype(jnp.bfloat16).reshape(mp_count, -1, fc1_weight.shape[1])
+        first_partial.astype(jnp.bfloat16).reshape(mp_count, -1, fc1_weight.shape[1]),
+        1,
     )
     hidden_part = jax.nn.gelu(
         first_total + fc1_bias.astype(jnp.float32), approximate=False

time: 271 us -> 240 us (0.89)
  waiting for transfers between devices: 174 us -> 0.01 us
  Pallas kernels: 0 us -> 155 us
  between operations: 14 us -> 0.89 us
  blocking collectives: 10.7 us -> 0 us
  other arithmetic: 16.9 us -> 22.8 us
    pallas_call x0 -> x6, Pallas kernels: none -> 155 us  [vmem_call(): pl.pallas_call(kernel, out_shape=out, in_specs=[pl.BlockSpec(memory_space...]
    all_gather x2 -> x0, waiting for transfers between devices: 60.1 us -> none  [the longest x1 31.3 us: gather_mp(): return lax.all_gather(value, 'mp', axis=0, tiled=True)]
    reduce_scatter x3 -> x0, waiting for transfers between devices: 59.4 us -> none  [the longest x2 59.4 us: sum_scatter_mp(): lax.psum_scatter(blocks, 'mp', scatter_dimension=0, tiled=False)]
    all_to_all x1, waiting for transfers between devices: 54 us -> 0.01 us  [per_device(): lax.all_to_all(send_place, ('section', 'dp'), split_axis=0, concat_axis=0...]
    psum x1 -> x0, blocking collectives: 10.7 us -> none  [total_mp(): return lax.psum(value, 'mp')]
    reduce_sum x0 -> x3, other arithmetic: none -> 4.69 us  [the longest x2 3.98 us: sum_scatter_mp(): return jnp.sum(exchange_mp(blocks, True, ident).astype(jnp.float32), axis=0)]
  transfers between devices with their start and end apart: 7 -> 2, of which waited for: 5 -> 0; matrix products, arithmetic and copies ran while one was open for 4% -> 24% of each run, Pallas kernels for 0% -> 60%
where the time goes in v2:
time: 240 us; the launch traced here: 239 us
  Pallas kernels  155 us (65%)
  matrix products  28.4 us (12%)
  other arithmetic  22.8 us (10%)
  local copies, waits for them, and re-layouts  21.3 us (9%)
  starting transfers between devices  10.5 us (4%)
    pallas_call x6, Pallas kernels, vmem_call(): pl.pallas_call(kernel, out_shape=out, in_specs=[pl.BlockSpec(memory_space...  155 us
    dot_general x1, matrix products, per_device(): jnp.dot(hidden, fc2_weight, preferred_element_type=jnp.float32)  6.29 us
    reshape x2, local copies, waits for them, and re-layouts, per_device(): partial_proj.astype(jnp.bfloat16).reshape(merged_rows, 4, width)  5.99 us
    ppermute x1, starting transfers between devices, from_behind(): lax.ppermute(value, axis, [(source, source + steps) for source in range(f...  5.26 us
    all_to_all x1, starting transfers between devices, per_device(): lax.all_to_all(send_place, ('section', 'dp'), split_axis=0, concat_axis=0...  5.2 us
    dot_general x1, matrix products, per_device(): jnp.dot(hits.astype(jnp.bfloat16), image_embeds, preferred_element_type=j...  4.97 us
  transfers between devices with their start and end apart: 2, of which 0 were waited for; matrix products, arithmetic and copies ran while one was open for 24% of the time, Pallas kernels for 60%

profile of v2, /device:TPU:0, one launch (start us, length us, event | category | flops | bytes accessed | tf_op | source)
XLA Modules:
  0.0 239.1 jit_solution(8423449556304722480)
XLA Ops:
  0.6 0.0 copy-start
  0.6 0.9 reshape.265
  1.5 0.1 slice_reduce_fusion
  1.7 1.3 fusion.50
  3.0 2.0 compare_select_fusion.2
  5.0 0.1 broadcast_in_dim.46
  5.0 0.1 select_reduce_fusion
  5.1 0.6 broadcast_add_fusion
  5.7 5.2 %all-to-all-start = ((s32[8,1,16]{2,1,0:T(1,128)}), s32[8,1,16]{2,1,0:T(1,128)}, u32[]{:S(2)}, u32[]{:S(2)}) async-start(s32[8,1,16]{2,1,0:T(1,128)} %bitcast.3), calls=%async_computation | async-start | bytes 8192 | tf_op jit(solution)/shard_map/all_to_all | solution.py:332
  10.9 5.3 %collective-permute-start = (bf16[512,2048]{1,0:T(8,128)(2,1)}, bf16[512,2048]{1,0:T(8,128)(2,1)}, u32[]{:S(2)}, u32[]{:S(2)}) collective-permute-start(bf16[512,2048]{1,0:T(8,128)(2,1)} %param.28), channel_id=1, source_target_pairs={{0,16},{1,17},{2,18},{3,19},{4,20},{5,21},{6,22},{7,23},{8,24},{9,... | collective-permute-start | bytes 6291464 | tf_op jit(solution)/shard_map/ppermute | solution.py:22
  16.2 0.7 iota_compare_fusion.4
  16.9 1.6 convert_reduce_fusion
  18.5 0.0 copy-start.1
  18.5 3.5 %reshape.266 = bf16[128,4,1280]{2,1,0:T(4,128)(2,1)} reshape(bf16[512,1280]{1,0:T(8,128)(2,1)} %param.16) | data formatting | bytes 2621440 | tf_op jit(solution)/shard_map/reshape | solution.py:358
  22.0 1.8 fusion.7
  23.8 0.0 copy-done.1
  23.8 4.7 %convolution_convert_fusion.5 = bf16[512,960]{0,1:T(8,128)(2,1)} fusion(bf16[1280,960]{0,1:T(8,128)(2,1)} %bitcast.83, bf16[512,1280]{1,0:T(8,128)(2,1)} %param.16, f32[1280]{0:T(1024)S(1)} %convert_element_type.97, f32[512]{0:T(512)S(1)} %add_rsqrt_fusion, f32[512]{0:T(512)S(1)} %broadcast_multiply_fusion), kind=kOutput, calls=%fused_computation.26 | convolution fusion | flops 1262059520 | bytes 4760576 | tf_op jit(solution)/shard_map/dot_general | solution.py:335
  28.5 3.3 %reshape.268 = bf16[2,256,3,4,80]{1,0,4,3,2:T(2,128)(2,1)} reshape(bf16[512,960]{0,1:T(8,128)(2,1)} %convolution_convert_fusion.5) | data formatting | bytes 1966080 | tf_op jit(solution)/shard_map/reshape | solution.py:338
  31.7 2.7 %fusion.49 = (bf16[2,256,1,4,80]{1,0,4,3,2:T(2,128)(2,1)S(1)}, bf16[2,256,1,4,80]{1,0,4,3,2:T(2,128)(2,1)S(1)}, bf16[2,256,1,4,80]{1,0,4,3,2:T(2,128)(2,1)}) fusion(bf16[2,256,3,4,80]{1,0,4,3,2:T(2,128)(2,1)} %reshape.268), kind=kLoop, calls=%fused_computation.104 | loop fusion | bytes 1966080 | tf_op jit(solution)/shard_map/slice | solution.py:341
  34.5 3.2 %fusion.51 = (f32[2,4,256]{2,1,0:T(4,128)S(1)}, f32[2,4,256,256]{2,3,1,0:T(8,128)}) fusion(pred[2,256]{1,0:T(4,128)(4,1)S(1)} %iota_compare_fusion.4, bf16[2,256,1,4,80]{1,0,4,3,2:T(2,128)(2,1)} %get-tuple-element.18, bf16[2,256,1,4,80]{1,0,4,3,2:T(2,128)(2,1)S(1)} %get-tuple-element.17), kind=kOutput, calls=%fused_computation.106 | convolution fusion | flops 85983488 | bytes 2761216 | tf_op jit(solution)/shard_map/sub | solution.py:350
  37.6 0.0 copy-start.7
  37.6 2.0 fusion.15
  39.6 0.3 copy.43
  40.0 0.0 copy-done.7
  40.0 1.9 convolution_convert_fusion.2
  42.0 3.5 %reshape.270 = bf16[128,4,1280]{2,1,0:T(4,128)(2,1)} reshape(bf16[512,1280]{1,0:T(8,128)(2,1)} %convolution_convert_fusion.2) | data formatting | bytes 2621440 | tf_op jit(solution)/shard_map/reshape | solution.py:361
  45.4 2.5 %copy.82 = bf16[128,4,1280]{2,0,1:T(8,128)(2,1)} copy(bf16[128,4,1280]{2,1,0:T(4,128)(2,1)} %reshape.270) | data formatting | bytes 2621440 | tf_op jit(solution)/shard_map/reshape | solution.py:361
  47.9 28.2 %shard_map.149 = bf16[4,128,1280]{2,1,0:T(8,128)(2,1)} custom-call(bf16[4,128,1280]{2,1,0:T(8,128)(2,1)} %bitcast.80), custom_call_target="tpu_custom_call" | custom-call | flops 26214400000 | bytes 2621440 | tf_op jit(solution)/shard_map/pallas_call | solution.py:37
  76.2 2.4 %convert_reduce_fusion.2 = f32[128,1280]{1,0:T(8,128)} fusion(bf16[4,128,1280]{2,1,0:T(8,128)(2,1)} %shard_map.149), kind=kLoop, calls=%fused_computation.18 | loop fusion | flops 1146880 | bytes 1966080 | tf_op jit(solution)/shard_map/reduce_sum | solution.py:100
  78.6 1.9 dynamic-slice_convert_fusion
  80.5 1.2 convert_reduce_fusion.3
  81.7 0.2 fusion.20
  82.0 0.1 broadcast_and_fusion
  82.1 0.2 and.61
  82.4 0.0 copy-done.2
  82.4 2.1 convolution_convert_fusion.3.x_ref
  84.5 19.1 %shard_map.150 = bf16[8,128,1280]{2,1,0:T(8,128)(2,1)} custom-call(bf16[128,1280]{1,0:T(8,128)(2,1)} %convolution_convert_fusion.3.x_ref), custom_call_target="tpu_custom_call" | custom-call | flops 52428800000 | bytes 5242880 | tf_op jit(solution)/shard_map/pallas_call | solution.py:37
  103.7 0.0 copy-start.6
  103.7 2.1 copy.46
  105.8 0.1 copy-done.6
  105.9 3.3 %convolution_convert_fusion.4 = bf16[1024,640]{1,0:T(8,128)(2,1)} fusion(bf16[1024,1280]{1,0:T(8,128)(2,1)S(1)} %bitcast.79, bf16[1280,640]{1,0:T(8,128)(2,1)S(1)} %copy-done.6), kind=kOutput, calls=%fused_computation.25 | convolution fusion | flops 1678376960 | bytes 5570560 | tf_op jit(solution)/shard_map/dot_general | solution.py:380
  109.1 0.0 copy-start.5
  109.1 34.0 %shard_map.151 = bf16[4,256,640]{2,1,0:T(8,128)(2,1)} custom-call(bf16[4,256,640]{2,1,0:T(8,128)(2,1)} %bitcast.85), custom_call_target="tpu_custom_call" | custom-call | flops 26214400000 | bytes 2621440 | tf_op jit(solution)/shard_map/pallas_call | solution.py:37
  143.2 1.6 convert_reduce_fusion.1
  144.7 0.0 copy-done.5
  144.8 2.2 fusion.23.x_ref
  146.9 32.8 %shard_map.152 = bf16[4,256,640]{2,1,0:T(8,128)(2,1)} custom-call(bf16[256,640]{1,0:T(8,128)(2,1)} %fusion.23.x_ref), custom_call_target="tpu_custom_call" | custom-call | flops 26214400000 | bytes 2621440 | tf_op jit(solution)/shard_map/pallas_call | solution.py:37
  179.7 0.0 copy-done
  179.7 6.3 %convolution_convert_fusion = bf16[1024,2048]{1,0:T(8,128)(2,1)} fusion(bf16[1024,640]{1,0:T(8,128)(2,1)} %bitcast.86, bf16[640,2048]{1,0:T(8,128)(2,1)S(1)} %copy-done), kind=kOutput, calls=%fused_computation.6 | convolution fusion | flops 2686451712 | bytes 8126464 | tf_op jit(solution)/shard_map/dot_general | solution.py:390
  186.0 0.0 copy-start.3
  186.0 0.0 copy-start.4
  186.0 29.3 %shard_map.153 = f32[128,2048]{1,0:T(8,128)} custom-call(bf16[8,128,2048]{2,1,0:T(8,128)(2,1)} %bitcast.84), custom_call_target="tpu_custom_call" | custom-call | flops 83886080000 | bytes 8388608 | tf_op jit(solution)/shard_map/pallas_call | solution.py:37
  215.3 0.0 copy-done.3
  215.3 0.0 copy-done.4
  215.3 0.0 all-to-all-done
  215.3 0.5 broadcast.247
  215.8 1.3 reduce.7
  217.2 0.1 eq.62
  217.3 0.2 fusion.41
  217.4 0.0 collective-permute-done
  217.4 5.0 %fusion.1 = (f32[512]{0:T(512)}, bf16[512,2048]{1,0:T(8,128)(2,1)}) fusion(bf16[512,2048]{1,0:T(8,128)(2,1)} %collective-permute-done, pred[]{:T(512)S(6)} %eq.69, bf16[512,2048]{1,0:T(8,128)(2,1)} %param.27, f32[128,2048]{1,0:T(8,128)} %shard_map.153, f32[2048]{0:T(1024)S(1)} %convert_element_type.120, s32[128]{0:T(128)S(1)} %eq.62, ...), kind=kOutput, calls=%fused_computation.3 | convolution fusion | flops 275316224 | bytes 7351297 | tf_op jit(solution)/shard_map/dot_general | solution.py:394
  222.4 11.9 %shard_map.154 = f32[4,4,128]{2,1,0:T(4,128)} custom-call(f32[4,128]{1,0:T(4,128)} %bitcast.87), custom_call_target="tpu_custom_call" | custom-call | flops 163840000 | bytes 16384 | tf_op jit(solution)/shard_map/pallas_call | solution.py:37
  234.3 0.7 reduce_sum.102
  235.0 4.1 %fusion.3 = bf16[512,2048]{1,0:T(8,128)(2,1)} fusion(f32[2048]{0:T(1024)S(1)} %convert_element_type.124, f32[512]{0:T(512)S(1)} %rsqrt_bitcast_fusion, bf16[512,2048]{1,0:T(8,128)(2,1)} %get-tuple-element.24, bf16[512,2048]{1,0:T(8,128)(2,1)} %collective-permute-done, pred[]{:T(512)S(6)} %eq.69), kind=kLoop, calls=%fused_computation.5 | loop fusion | flops 5242880 | bytes 6301697 | tf_op jit(solution)/shard_map/convert_element_type | solution.py:404
  (15 shorter events, 0.1 us)
Async XLA Ops:
  0.6 179.1 %copy-start = (bf16[640,2048]{1,0:T(8,128)(2,1)S(1)}, bf16[640,2048]{1,0:T(8,128)(2,1)}, u32[]{:S(2)}) copy-start(bf16[640,2048]{1,0:T(8,128)(2,1)} %param.25) | copy-start | bytes 7864324
  5.7 209.6 %all-to-all-start = ((s32[8,1,16]{2,1,0:T(1,128)}), s32[8,1,16]{2,1,0:T(1,128)}, u32[]{:S(2)}, u32[]{:S(2)}) async-start(s32[8,1,16]{2,1,0:T(1,128)} %bitcast.3), calls=%async_computation | async-start | bytes 8192 | tf_op jit(solution)/shard_map/all_to_all | solution.py:332
  10.9 206.5 %collective-permute-start = (bf16[512,2048]{1,0:T(8,128)(2,1)}, bf16[512,2048]{1,0:T(8,128)(2,1)}, u32[]{:S(2)}, u32[]{:S(2)}) collective-permute-start(bf16[512,2048]{1,0:T(8,128)(2,1)} %param.28), channel_id=1, source_target_pairs={{0,16},{1,17},{2,18},{3,19},{4,20},{5,21},{6,22},{7,23},{8,24},{9,... | collective-permute-start | bytes 6291464 | tf_op jit(solution)/shard_map/ppermute | solution.py:22
  18.5 5.3 %copy-start.1 = (bf16[1280]{0:T(1024)(128)(2,1)S(1)}, bf16[1280]{0:T(1024)(128)(2,1)}, u32[]{:S(2)}) copy-start(bf16[1280]{0:T(1024)(128)(2,1)} %param.21) | copy-start | bytes 7684
  37.6 2.4 copy-start.7
  78.6 3.8 %copy-start.2 = (bf16[1280]{0:T(1024)(128)(2,1)S(1)}, bf16[1280]{0:T(1024)(128)(2,1)}, u32[]{:S(2)}) copy-start(bf16[1280]{0:T(1024)(128)(2,1)} %param.22) | copy-start | bytes 7684
  103.7 2.2 copy-start.6
  109.1 35.6 %copy-start.5 = (bf16[640]{0:T(1024)(128)(2,1)S(1)}, bf16[640]{0:T(1024)(128)(2,1)}, u32[]{:S(2)}) copy-start(bf16[640]{0:T(1024)(128)(2,1)} %param.24) | copy-start | bytes 3844
  186.0 29.3 %copy-start.3 = (bf16[2048]{0:T(1024)(128)(2,1)S(1)}, bf16[2048]{0:T(1024)(128)(2,1)}, u32[]{:S(2)}) copy-start(bf16[2048]{0:T(1024)(128)(2,1)} %param.26) | copy-start | bytes 12292
  186.0 29.3 %copy-start.4 = (bf16[2048]{0:T(1024)(128)(2,1)S(1)}, bf16[2048]{0:T(1024)(128)(2,1)}, u32[]{:S(2)}) copy-start(bf16[2048]{0:T(1024)(128)(2,1)} %param.29) | copy-start | bytes 12292

commit v3 on v2

--- a/solution.py
+++ b/solution.py
@@ -78,6 +78,82 @@
         copy.wait()
 
 
+def relay_kernel(count, x_ref, o_ref, send_sem, recv_sem, own_sem):
+    me = lax.axis_index("mp")
+    barrier = pltpu.get_barrier_semaphore()
+    for step in range(1, count):
+        peer = lax.rem(me + step, count)
+        pl.semaphore_signal(
+            barrier, inc=1, device_id={"mp": peer}, device_id_type=pl.DeviceIdType.MESH
+        )
+    pl.semaphore_wait(barrier, count - 1)
+    own = pltpu.make_async_copy(x_ref, o_ref.at[me], own_sem)
+    own.start()
+
+    def hop(way, step):
+        owner = lax.rem(me - way * step + count, count)
+        return pltpu.make_async_remote_copy(
+            src_ref=o_ref.at[owner] if step else x_ref,
+            dst_ref=o_ref.at[owner],
+            send_sem=send_sem.at[(way + 1) // 2, step],
+            recv_sem=recv_sem.at[(way + 1) // 2, step],
+            device_id={"mp": lax.rem(me + way + count, count)},
+            device_id_type=pl.DeviceIdType.MESH,
+        )
+
+    def holds(way, step):
+        return me >= step if way > 0 else me + step < count
+
+    def sends(way):
+        return me < count - 1 if way > 0 else me > 0
+
+    for step in range(count):
+        for way in (1, -1):
+            if step:
+
+                @pl.when(holds(way, step))
+                def _():
+                    owner = lax.rem(me - way * step + count, count)
+                    pltpu.make_async_remote_copy(
+                        src_ref=x_ref,
+                        dst_ref=o_ref.at[owner],
+                        send_sem=send_sem.at[(way + 1) // 2, step - 1],
+                        recv_sem=recv_sem.at[(way + 1) // 2, step - 1],
+                        device_id={"mp": lax.rem(me - way + count, count)},
+                        device_id_type=pl.DeviceIdType.MESH,
+                    ).wait_recv()
+
+            if step < count - 1:
+
+                @pl.when(jnp.logical_and(holds(way, step), sends(way)))
+                def _():
+                    hop(way, step).start()
+
+    own.wait()
+    for step in range(count - 1):
+        for way in (1, -1):
+
+            @pl.when(jnp.logical_and(holds(way, step), sends(way)))
+            def _():
+                hop(way, step).wait_send()
+
+
+def relay_mp(value, ident):
+    count = lax.axis_size("mp")
+    return vmem_call(
+        functools.partial(relay_kernel, count),
+        jax.ShapeDtypeStruct((count,) + value.shape, value.dtype),
+        [
+            pltpu.SemaphoreType.DMA((2, count - 1)),
+            pltpu.SemaphoreType.DMA((2, count - 1)),
+            pltpu.SemaphoreType.DMA,
+        ],
+        count * value.size * value.dtype.itemsize,
+        ident,
+        value,
+    )
+
+
 def exchange_mp(value, spread, ident):
     count = lax.axis_size("mp")
     shape = value.shape if spread else (count,) + value.shape
@@ -101,7 +177,7 @@
 
 
 def gather_mp(value):
-    got = exchange_mp(value, False, 2)
+    got = relay_mp(value, 2)
     return got.reshape((-1,) + value.shape[1:])
 
 
@@ -352,24 +428,27 @@
         "thqk,tkhd->tqhd", weights, value_part, preferred_element_type=jnp.float32
     ).astype(jnp.bfloat16)
     attended = attended.reshape(patches.shape[0], local_cols)
-    partial_proj = jnp.dot(attended, out_weight, preferred_element_type=jnp.float32)
-    position = lax.axis_index("mp")
-    own_patch = lax.dynamic_slice_in_dim(
-        patches.reshape(merged_rows, 4, width), position, 1, 1
-    ).reshape(merged_rows, width)
+    lane_source = jnp.arange(run_total, dtype=jnp.int32)[None, :] * run_cap
+    run_source = jnp.sum(jnp.where(takes, lane_source, 0), axis=1)
+    row_source = (
+        run_source[:, None] + jnp.arange(run_cap, dtype=jnp.int32)[None, :]
+    ).reshape(-1) * 4
+    slots_at = jnp.arange(patches.shape[0], dtype=jnp.int32)
+    patch_at = jnp.arange(4, dtype=jnp.int32)
+    order = (
+        (row_source[None, :] + patch_at[:, None]).reshape(-1)[:, None] == slots_at[None, :]
+    ).astype(jnp.bfloat16)
+    own_order = (
+        (row_source + lax.axis_index("mp"))[:, None] == slots_at[None, :]
+    ).astype(jnp.bfloat16)
+    ordered = jnp.dot(order, attended, preferred_element_type=jnp.float32).astype(jnp.bfloat16)
+    own_patch = jnp.dot(own_order, patches, preferred_element_type=jnp.float32)
+    partial_proj = jnp.dot(ordered, out_weight, preferred_element_type=jnp.float32)
     own_proj = sum_scatter_mp(
-        partial_proj.astype(jnp.bfloat16).reshape(merged_rows, 4, width).transpose(1, 0, 2),
-        0,
-    )
-    block_out = (own_patch.astype(jnp.float32) + own_proj).astype(jnp.bfloat16)
+        partial_proj.astype(jnp.bfloat16).reshape(4, group_count * run_cap, width), 0
+    )
+    block_out = (own_patch + own_proj).astype(jnp.bfloat16)
     merge_part = layer_norm(block_out, merge_gain).astype(jnp.bfloat16)
-    lane_same = jnp.arange(run_cap)[:, None] == jnp.arange(run_cap)[None, :]
-    order = (takes[:, None, :, None] & lane_same[None, :, None, :]).reshape(
-        group_count * run_cap, merged_rows
-    )
-    merge_part = jnp.dot(
-        order.astype(jnp.bfloat16), merge_part, preferred_element_type=jnp.float32
-    ).astype(jnp.bfloat16)
     slot_rows = group_count * run_cap
     gathered = gather_groups(merge_part)
     gathered = (

time: 240 us -> 222 us (0.925)
  local copies, waits for them, and re-layouts: 21.3 us -> 11.6 us
  Pallas kernels: 155 us -> 150 us
  other arithmetic: 22.8 us -> 18.4 us
    reshape x3 -> x0, local copies, waits for them, and re-layouts: 9.49 us -> none  [the longest x2 5.99 us: per_device(): partial_proj.astype(jnp.bfloat16).reshape(merged_rows, 4, width)]
    pallas_call x6, Pallas kernels: 155 us -> 150 us  [vmem_call(): pl.pallas_call(kernel, out_shape=out, in_specs=[pl.BlockSpec(memory_space...]
  transfers between devices with their start and end apart: 2 -> 2, of which waited for: 0 -> 0; matrix products, arithmetic and copies ran while one was open for 24% -> 20% of each run, Pallas kernels for 60% -> 65%
where the time goes in v3:
time: 222 us; the launch traced here: 221 us
  Pallas kernels  150 us (68%)
  matrix products  29.1 us (13%)
  other arithmetic  18.4 us (8%)
  local copies, waits for them, and re-layouts  11.6 us (5%)
  starting transfers between devices  10.6 us (5%)
    pallas_call x6, Pallas kernels, vmem_call(): pl.pallas_call(kernel, out_shape=out, in_specs=[pl.BlockSpec(memory_space...  150 us
    dot_general x1, matrix products, per_device(): jnp.dot(hidden, fc2_weight, preferred_element_type=jnp.float32)  6.29 us
    ppermute x1, starting transfers between devices, from_behind(): lax.ppermute(value, axis, [(source, source + steps) for source in range(f...  5.38 us
    all_to_all x1, starting transfers between devices, per_device(): lax.all_to_all(send_place, ('section', 'dp'), split_axis=0, concat_axis=0...  5.2 us
    dot_general x1, matrix products, per_device(): jnp.dot(hits.astype(jnp.bfloat16), image_embeds, preferred_element_type=j...  4.97 us
  transfers between devices with their start and end apart: 2, of which 0 were waited for; matrix products, arithmetic and copies ran while one was open for 20% of the time, Pallas kernels for 65%

profile of v3, /device:TPU:0, one launch (start us, length us, event | category | flops | bytes accessed | tf_op | source)
XLA Modules:
  0.0 221.2 jit_solution(15574821456396241994)
XLA Ops:
  0.6 0.0 copy-start
  0.6 0.0 copy-start.2
  0.7 0.9 reshape.244
  1.5 0.1 slice_reduce_fusion
  1.7 1.3 fusion.44
  3.0 2.0 compare_select_fusion.2
  5.0 0.1 broadcast_in_dim.58
  5.1 0.1 select_reduce_fusion
  5.2 0.6 broadcast_add_fusion
  5.7 5.2 %all-to-all-start = ((s32[8,1,16]{2,1,0:T(1,128)}), s32[8,1,16]{2,1,0:T(1,128)}, u32[]{:S(2)}, u32[]{:S(2)}) async-start(s32[8,1,16]{2,1,0:T(1,128)} %bitcast.3), calls=%async_computation | async-start | bytes 8192 | tf_op jit(solution)/shard_map/all_to_all | solution.py:408
  10.9 0.0 copy-start.1
  10.9 5.4 %collective-permute-start = (bf16[512,2048]{1,0:T(8,128)(2,1)}, bf16[512,2048]{1,0:T(8,128)(2,1)}, u32[]{:S(2)}, u32[]{:S(2)}) collective-permute-start(bf16[512,2048]{1,0:T(8,128)(2,1)} %param.28), channel_id=1, source_target_pairs={{0,16},{1,17},{2,18},{3,19},{4,20},{5,21},{6,22},{7,23},{8,24},{9,... | collective-permute-start | bytes 6291464 | tf_op jit(solution)/shard_map/ppermute | solution.py:22
  16.3 0.7 iota_compare_fusion.8
  17.1 1.6 convert_reduce_fusion
  18.6 0.0 copy-done.1
  18.6 0.5 fusion.7
  19.1 0.0 copy-done.2
  19.1 4.3 %convolution_convert_fusion.4 = bf16[512,960]{0,1:T(8,128)(2,1)} fusion(bf16[1280,960]{0,1:T(8,128)(2,1)} %bitcast.65, bf16[512,1280]{1,0:T(8,128)(2,1)S(1)} %copy-done.1, f32[1280]{0:T(1024)S(1)} %convert_element_type.79, f32[512]{0:T(512)S(1)} %add_rsqrt_fusion, f32[512]{0:T(512)S(1)} %broadcast_multiply_fusion), kind=kOutput, calls=%fused_computation.28 | convolution fusion | flops 1262059520 | bytes 4760576 | tf_op jit(solution)/shard_map/dot_general | solution.py:411
  23.4 3.3 %reshape.246 = bf16[2,256,3,4,80]{1,0,4,3,2:T(2,128)(2,1)} reshape(bf16[512,960]{0,1:T(8,128)(2,1)} %convolution_convert_fusion.4) | data formatting | bytes 1966080 | tf_op jit(solution)/shard_map/reshape | solution.py:414
  26.7 2.7 %fusion.43 = (bf16[2,256,1,4,80]{1,0,4,3,2:T(2,128)(2,1)S(1)}, bf16[2,256,1,4,80]{1,0,4,3,2:T(2,128)(2,1)S(1)}, bf16[2,256,1,4,80]{1,0,4,3,2:T(2,128)(2,1)}) fusion(bf16[2,256,3,4,80]{1,0,4,3,2:T(2,128)(2,1)} %reshape.246), kind=kLoop, calls=%fused_computation.101 | loop fusion | bytes 1966080 | tf_op jit(solution)/shard_map/slice | solution.py:417
  29.4 3.2 %fusion.45 = (f32[2,4,256]{2,1,0:T(4,128)S(1)}, f32[2,4,256,256]{2,3,1,0:T(8,128)}) fusion(pred[2,256]{1,0:T(4,128)(4,1)S(1)} %iota_compare_fusion.8, bf16[2,256,1,4,80]{1,0,4,3,2:T(2,128)(2,1)} %get-tuple-element.16, bf16[2,256,1,4,80]{1,0,4,3,2:T(2,128)(2,1)S(1)} %get-tuple-element.15), kind=kOutput, calls=%fused_computation.103 | convolution fusion | flops 85983488 | bytes 2761216 | tf_op jit(solution)/shard_map/sub | solution.py:426
  32.6 1.9 fusion.17
  34.5 0.3 copy.38
  34.8 0.1 select_reduce_fusion.1
  35.0 0.1 add_multiply_fusion
  35.0 0.1 mul.106
  35.1 3.5 %convolution_convert_fusion.2 = bf16[512,1280]{1,0:T(8,128)(2,1)} fusion(bf16[320,1280]{1,0:T(8,128)(2,1)} %param.20, bf16[512,320]{0,1:T(8,128)(2,1)S(1)} %bitcast.64, s32[512]{0:T(512)S(1)} %add_bitcast_fusion), kind=kOutput, calls=%fused_computation.12 | convolution fusion | flops 588283904 | bytes 2459648 | tf_op jit(solution)/shard_map/dot_general | solution.py:446
  38.6 28.2 %shard_map.149 = bf16[4,128,1280]{2,1,0:T(8,128)(2,1)} custom-call(bf16[4,128,1280]{2,1,0:T(8,128)(2,1)} %bitcast.67), custom_call_target="tpu_custom_call" | custom-call | flops 26214400000 | bytes 2621440 | tf_op jit(solution)/shard_map/pallas_call | solution.py:37
  66.8 1.6 convert_reduce_fusion.2
  68.4 0.0 copy-start.3
  68.4 1.8 fusion.46
  70.2 0.2 multiply_reduce_fusion
  70.4 0.0 copy-done.3
  70.5 0.9 multiply_convert_fusion.x_ref
  71.4 19.1 %shard_map.150 = bf16[8,128,1280]{2,1,0:T(8,128)(2,1)} custom-call(bf16[128,1280]{1,0:T(8,128)(2,1)} %multiply_convert_fusion.x_ref), custom_call_target="tpu_custom_call" | custom-call | flops 52428800000 | bytes 5242880 | tf_op jit(solution)/shard_map/pallas_call | solution.py:37
  90.5 0.0 copy-start.7
  90.5 2.1 copy.39
  92.6 0.1 copy-done.7
  92.7 3.3 %convolution_convert_fusion.3 = bf16[1024,640]{1,0:T(8,128)(2,1)} fusion(bf16[1024,1280]{1,0:T(8,128)(2,1)S(1)} %bitcast.62, bf16[1280,640]{1,0:T(8,128)(2,1)S(1)} %copy-done.7), kind=kOutput, calls=%fused_computation.27 | convolution fusion | flops 1678376960 | bytes 5570560 | tf_op jit(solution)/shard_map/dot_general | solution.py:459
  96.0 0.0 copy-start.6
  96.0 34.0 %shard_map.151 = bf16[4,256,640]{2,1,0:T(8,128)(2,1)} custom-call(bf16[4,256,640]{2,1,0:T(8,128)(2,1)} %bitcast.68), custom_call_target="tpu_custom_call" | custom-call | flops 26214400000 | bytes 2621440 | tf_op jit(solution)/shard_map/pallas_call | solution.py:37
  130.0 1.6 convert_reduce_fusion.1
  131.6 0.0 copy-done.6
  131.6 2.2 fusion.23.x_ref
  133.7 32.9 %shard_map.152 = bf16[4,256,640]{2,1,0:T(8,128)(2,1)} custom-call(bf16[256,640]{1,0:T(8,128)(2,1)} %fusion.23.x_ref), custom_call_target="tpu_custom_call" | custom-call | flops 26214400000 | bytes 2621440 | tf_op jit(solution)/shard_map/pallas_call | solution.py:37
  166.6 0.0 copy-done
  166.6 6.3 %convolution_convert_fusion = bf16[1024,2048]{1,0:T(8,128)(2,1)} fusion(bf16[1024,640]{1,0:T(8,128)(2,1)} %bitcast.69, bf16[640,2048]{1,0:T(8,128)(2,1)S(1)} %copy-done), kind=kOutput, calls=%fused_computation.6 | convolution fusion | flops 2686451712 | bytes 8126464 | tf_op jit(solution)/shard_map/dot_general | solution.py:469
  172.9 0.0 copy-start.4
  172.9 0.0 copy-start.5
  172.9 29.5 %shard_map.153 = f32[128,2048]{1,0:T(8,128)} custom-call(bf16[8,128,2048]{2,1,0:T(8,128)(2,1)} %bitcast.66), custom_call_target="tpu_custom_call" | custom-call | flops 83886080000 | bytes 8388608 | tf_op jit(solution)/shard_map/pallas_call | solution.py:37
  202.5 0.0 copy-done.4
  202.5 0.0 copy-done.5
  202.5 0.0 all-to-all-done
  202.5 0.5 broadcast.253
  203.0 1.3 reduce.7
  204.4 0.1 eq.67
  204.5 0.2 fusion.35
  204.6 0.0 collective-permute-done
  204.6 5.0 %fusion.1 = (f32[512]{0:T(512)}, bf16[512,2048]{1,0:T(8,128)(2,1)}) fusion(bf16[512,2048]{1,0:T(8,128)(2,1)} %collective-permute-done, pred[]{:T(512)S(6)} %eq.77, bf16[512,2048]{1,0:T(8,128)(2,1)} %param.27, f32[128,2048]{1,0:T(8,128)} %shard_map.153, f32[2048]{0:T(1024)S(1)} %convert_element_type.97, s32[128]{0:T(128)S(1)} %eq.67, ...), kind=kOutput, calls=%fused_computation.3 | convolution fusion | flops 275316224 | bytes 7351297 | tf_op jit(solution)/shard_map/dot_general | solution.py:473
  209.6 6.7 %shard_map.154 = f32[4,4,128]{2,1,0:T(4,128)} custom-call(f32[4,128]{1,0:T(4,128)} %bitcast.70), custom_call_target="tpu_custom_call" | custom-call | flops 163840000 | bytes 16384 | tf_op jit(solution)/shard_map/pallas_call | solution.py:37
  216.4 0.7 reduce_sum.109
  217.1 4.1 %fusion.3 = bf16[512,2048]{1,0:T(8,128)(2,1)} fusion(f32[2048]{0:T(1024)S(1)} %convert_element_type.101, f32[512]{0:T(512)S(1)} %rsqrt_bitcast_fusion, bf16[512,2048]{1,0:T(8,128)(2,1)} %get-tuple-element.24, bf16[512,2048]{1,0:T(8,128)(2,1)} %collective-permute-done, pred[]{:T(512)S(6)} %eq.77), kind=kLoop, calls=%fused_computation.5 | loop fusion | flops 5242880 | bytes 6301697 | tf_op jit(solution)/shard_map/convert_element_type | solution.py:483
  (15 shorter events, 0.1 us)
Async XLA Ops:
  0.6 166.0 %copy-start = (bf16[640,2048]{1,0:T(8,128)(2,1)S(1)}, bf16[640,2048]{1,0:T(8,128)(2,1)}, u32[]{:S(2)}) copy-start(bf16[640,2048]{1,0:T(8,128)(2,1)} %param.25) | copy-start | bytes 7864324
  0.6 18.5 %copy-start.2 = (bf16[1280]{0:T(1024)(128)(2,1)S(1)}, bf16[1280]{0:T(1024)(128)(2,1)}, u32[]{:S(2)}) copy-start(bf16[1280]{0:T(1024)(128)(2,1)} %param.21) | copy-start | bytes 7684
  5.7 196.8 %all-to-all-start = ((s32[8,1,16]{2,1,0:T(1,128)}), s32[8,1,16]{2,1,0:T(1,128)}, u32[]{:S(2)}, u32[]{:S(2)}) async-start(s32[8,1,16]{2,1,0:T(1,128)} %bitcast.3), calls=%async_computation | async-start | bytes 8192 | tf_op jit(solution)/shard_map/all_to_all | solution.py:408
  10.9 7.7 %copy-start.1 = (bf16[512,1280]{1,0:T(8,128)(2,1)S(1)}, bf16[512,1280]{1,0:T(8,128)(2,1)}, u32[]{:S(2)}) copy-start(bf16[512,1280]{1,0:T(8,128)(2,1)} %param.16) | copy-start | bytes 3932164
  10.9 193.7 %collective-permute-start = (bf16[512,2048]{1,0:T(8,128)(2,1)}, bf16[512,2048]{1,0:T(8,128)(2,1)}, u32[]{:S(2)}, u32[]{:S(2)}) collective-permute-start(bf16[512,2048]{1,0:T(8,128)(2,1)} %param.28), channel_id=1, source_target_pairs={{0,16},{1,17},{2,18},{3,19},{4,20},{5,21},{6,22},{7,23},{8,24},{9,... | collective-permute-start | bytes 6291464 | tf_op jit(solution)/shard_map/ppermute | solution.py:22
  68.4 2.0 copy-start.3
  90.5 2.2 %copy-start.7 = (bf16[1280,640]{1,0:T(8,128)(2,1)S(1)}, bf16[1280,640]{1,0:T(8,128)(2,1)}, u32[]{:S(2)}) copy-start(bf16[1280,640]{1,0:T(8,128)(2,1)} %param.23) | copy-start | bytes 4915204
  96.0 35.6 %copy-start.6 = (bf16[640]{0:T(1024)(128)(2,1)S(1)}, bf16[640]{0:T(1024)(128)(2,1)}, u32[]{:S(2)}) copy-start(bf16[640]{0:T(1024)(128)(2,1)} %param.24) | copy-start | bytes 3844
  172.9 29.5 %copy-start.4 = (bf16[2048]{0:T(1024)(128)(2,1)S(1)}, bf16[2048]{0:T(1024)(128)(2,1)}, u32[]{:S(2)}) copy-start(bf16[2048]{0:T(1024)(128)(2,1)} %param.26) | copy-start | bytes 12292
  172.9 29.6 %copy-start.5 = (bf16[2048]{0:T(1024)(128)(2,1)S(1)}, bf16[2048]{0:T(1024)(128)(2,1)}, u32[]{:S(2)}) copy-start(bf16[2048]{0:T(1024)(128)(2,1)} %param.29) | copy-start | bytes 12292
